TPU v7x, 512 devices: a whole 4x4x16 slice. The times are simulated.
512 devices in a mesh: tm: 8 (over z_hi, core), row: 16 (over z_lo, x), col: 4 (over y).
Axes of the slice: x: 4, y: 4, z: 16 (z_hi: 4, z_lo: 4; z = z_hi * 4 + z_lo), core: 2. Of those that a mesh axis runs over, the one named last changes fastest.
Arguments:
- occ_orbitals: bfloat16 [4096, 2048], P(('col', 'row'), 'tm'), may hold values from -0.4375 to 0.4375
- empty_orbitals: bfloat16 [4096, 2048], P(('col', 'row'), 'tm'), may hold values from -0.4375 to 0.4375
- occ_rate: float32 [2048], replicated, may hold values from 0.05 to 4
- empty_rate: float32 [2048], replicated, may hold values from 0.05 to 4
- columns: bfloat16 [4096, 256], P(('col', 'row')), may hold values from -6 to 6
Outputs:
- screened_columns: float32 [4096, 16, 256], P(('col', 'row'), 'tm')
All inputs are finite; a program needn't handle non-finite values.
Results may differ from a plain program's by a relative error of at most 0.018.
Values may be sent and summed in bfloat16 or wider, within the bound.
A program may use at most 64 MiB of HBM per device.

v0:
```python
import jax
import jax.numpy as jnp
from jax import lax
from jax.sharding import PartitionSpec as P

NT = 16
NF = 16


damping = 0.3


def sent_together(arrays, axis, dim, along):
    both = jnp.concatenate(arrays, axis=along)
    result, at, gathered = (lax.all_gather(both, axis, axis=dim, tiled=True), 0, [])
    for a in arrays:
        gathered.append(lax.slice_in_dim(result, at, at + a.shape[along], axis=along))
        at += a.shape[along]
    return tuple(gathered)


def sent_to_all(shard, axis):
    copies = jnp.broadcast_to(shard, (lax.axis_size(axis), *shard.shape))
    return lax.all_to_all(copies, axis, split_axis=0, concat_axis=0, tiled=True)


def of_everyone(shard, axis):
    return sent_to_all(shard, axis).astype(jnp.float32).sum(axis=0)


def split_up(shard, dim, size):
    before, after = (shard.shape[:dim], shard.shape[dim + 1 :])
    return jnp.moveaxis(shard.reshape(*before, size, -1, *after), dim, 0)


def sum_at_owner(shard, axis, dim):
    parts = split_up(shard, dim, lax.axis_size(axis))
    arrived = lax.all_to_all(parts, axis, split_axis=0, concat_axis=0, tiled=True)
    return arrived.astype(jnp.float32).sum(axis=0)


def time_tables(count_times, count_freqs):
    moments = 0.25 * (jnp.arange(count_times).astype(jnp.float32) + 0.5)
    omegas = 0.4 * (jnp.arange(count_freqs).astype(jnp.float32) + 0.5)
    cosine = (0.5 * jnp.cos(omegas[:, None] * moments[None, :])).astype(jnp.bfloat16)
    return (moments, cosine)


def shards(occ_orbitals, empty_orbitals, occ_rate, empty_rate, columns):
    tm_count = lax.axis_size("tm")
    occ_part, empty_part = sent_together((occ_orbitals, empty_orbitals), "tm", 1, 0)
    occ_block, empty_block, rhs_block = sent_together((occ_part, empty_part, columns), "row", 0, 1)
    shard_rows = occ_orbitals.shape[0]
    row_index = lax.axis_index("row")
    own_start = row_index * shard_rows
    own_occ = lax.dynamic_slice_in_dim(occ_block, own_start, shard_rows, 0)
    own_empty = lax.dynamic_slice_in_dim(empty_block, own_start, shard_rows, 0)
    occ_rows, empty_rows, rhs_rows = sent_together((own_occ, own_empty, columns), "col", 0, 1)
    moments, cosine = time_tables(NT, NF)
    local_times = NT // tm_count
    first_time = lax.axis_index("tm") * local_times
    occ_wide = occ_rows.astype(jnp.float32)
    empty_wide = empty_rows.astype(jnp.float32)
    tiles = []
    for step in range(local_times):
        moment = moments[first_time + step]
        scaled_occ = (occ_wide * jnp.exp(-occ_rate * moment)[None, :]).astype(jnp.bfloat16)
        scaled_empty = (empty_wide * jnp.exp(-empty_rate * moment)[None, :]).astype(jnp.bfloat16)
        green_occ = jnp.einsum(
            "ro,co->rc", scaled_occ, occ_block, preferred_element_type=jnp.float32
        )
        green_empty = jnp.einsum(
            "ro,co->rc", scaled_empty, empty_block, preferred_element_type=jnp.float32
        )
        tiles.append((-2.0 * green_occ * green_empty).astype(jnp.bfloat16))
    polar = jnp.stack(tiles)
    spectral = jnp.einsum(
        "kj,jrc->krc",
        cosine,
        lax.all_to_all(polar, "tm", split_axis=2, concat_axis=0, tiled=True),
        preferred_element_type=jnp.float32,
    ).astype(jnp.bfloat16)
    screened = lax.all_to_all(spectral, "tm", split_axis=0, concat_axis=2, tiled=True)
    partial_value = jnp.einsum(
        "frc,cn->frn", screened, rhs_block, preferred_element_type=jnp.float32
    )
    first = of_everyone(partial_value.astype(jnp.bfloat16), "col").astype(jnp.float32)
    middle = (rhs_rows.astype(jnp.float32)[None, :, :] + damping * first).astype(jnp.bfloat16)
    second = sum_at_owner(
        jnp.einsum("frc,frn->cfn", screened, middle, preferred_element_type=jnp.float32).astype(
            jnp.bfloat16
        ),
        "row",
        0,
    )
    return columns.astype(jnp.float32)[:, None, :] + damping * second


def solution(mesh):
    placed = (P(("col", "row"), "tm"), P(("col", "row"), "tm"), P(), P(), P(("col", "row"), None))
    return jax.shard_map(
        shards, mesh=mesh, in_specs=placed, out_specs=P(("col", "row"), "tm", None), check_vma=False
    )
```

profile of v0, /device:TPU:1, one launch (start us, length us, event | category | flops | bytes accessed | tf_op | source)
XLA Modules:
  0.0 384.2 jit_solution(8197709345672664914)
XLA Ops:
  6.5 0.0 all-gather.3.cloned.1.call-start
  6.5 0.8 pad_maximum_fusion.3
  7.3 29.1 %all_gather.9 = bf16[128,2048]{1,0:T(8,128)(2,1)S(1)} all-gather(bf16[128,256]{1,0:T(8,128)(2,1)S(1)} %pad_maximum_fusion.3), channel_id=1, replica_groups=mesh['tm'=8,'row'=16,'col'=4] {'tm'}, dimensions={1}, use_global_device_ids=true | all-gather | bytes 589824 | tf_op jit(solution)/shard_map/all_gather | solution.py:15
  36.5 1.6 pad_maximum_fusion.2
  38.1 0.0 all-gather.3.cloned.1.call-update
  38.1 0.0 all-gather.5.cloned.1.call-start
  38.2 0.0 copy-start.1
  38.2 108.2 %all-gather.3.cloned.1.call-done = bf16[1024,4352]{1,0:T(8,128)(2,1)} async-done(((bf16[64,4352]{1,0:T(8,128)(2,1)}), bf16[1024,4352]{1,0:T(8,128)(2,1)}) %all-gather.3.cloned.1.call-update) | async-done | bytes 8912912 | tf_op jit(solution)/shard_map/all_gather | solution.py:15
  146.4 4.0 %fusion.36 = (bf16[1024,2048]{1,0:T(8,128)(2,1)S(1)}, bf16[1024,2048]{1,0:T(8,128)(2,1)S(1)}) fusion(bf16[1024,4352]{1,0:T(8,128)(2,1)} %all-gather.3.cloned.1.call-done), kind=kLoop, calls=%fused_computation.61 | loop fusion | bytes 16777216 | tf_op jit(solution)/shard_map/slice | solution.py:17
  150.4 0.0 copy-start.2
  150.4 0.0 copy-start.3
  150.5 0.0 copy-done.1
  150.5 0.8 pad_maximum_fusion.1
  151.4 0.0 all-gather.5.cloned.1.call-update
  151.4 0.7 fusion.38
  152.1 0.0 copy-done.2
  152.1 0.0 copy-done.3
  152.1 1.3 multiply_exponential_fusion.2
  153.4 34.5 %all-gather.5.cloned.1.call-done = bf16[256,4352]{1,0:T(8,128)(2,1)} async-done(((bf16[64,4352]{1,0:T(8,128)(2,1)}), bf16[256,4352]{1,0:T(8,128)(2,1)}) %all-gather.5.cloned.1.call-update) | async-done | bytes 2228240 | tf_op jit(solution)/shard_map/all_gather | solution.py:15
  187.9 0.0 copy-start
  187.9 3.9 %convolution_multiply_fusion.3 = f32[256,1024]{1,0:T(8,128)S(1)} fusion(f32[2048]{0:T(1024)S(1)} %get-tuple-element.16, bf16[256,4352]{1,0:T(8,128)(2,1)} %all-gather.5.cloned.1.call-done, bf16[1024,4352]{1,0:T(8,128)(2,1)} %all-gather.3.cloned.1.call-done), kind=kOutput, calls=%fused_computation.16 | convolution fusion | flops 1075576832 | bytes 6299648 | tf_op jit(solution)/shard_map/ro,co->rc/dot_general | solution.py:69
  191.9 1.2 copy-done
  193.0 0.0 copy-start.4
  193.0 2.6 convolution_multiply_fusion.1
  195.7 0.0 copy-done.4
  195.7 1.3 fusion.8
  197.0 1.3 fusion.7
  198.3 0.1 pad_maximum_fusion
  198.4 2.0 copy.22
  200.4 13.0 %all-to-all-start = ((bf16[2,256,1024]{1,0,2:T(2,128)(2,1)}), bf16[2,256,1024]{1,0,2:T(2,128)(2,1)S(1)}, u32[]{:S(2)}, u32[]{:S(2)}) async-start(bf16[2,256,1024]{1,0,2:T(2,128)(2,1)} %copy.22), calls=%async_computation | async-start | bytes 2097152 | tf_op jit(solution)/shard_map/all_to_all | solution.py:80
  213.5 49.0 %all-to-all-done = bf16[2,256,1024]{1,0,2:T(2,128)(2,1)S(1)} async-done(((bf16[2,256,1024]{1,0,2:T(2,128)(2,1)}), bf16[2,256,1024]{1,0,2:T(2,128)(2,1)S(1)}, u32[]{:S(2)}, u32[]{:S(2)}) %all-to-all-start) | async-done | bytes 1048608 | tf_op jit(solution)/shard_map/all_to_all | solution.py:80
  262.4 2.5 copy.23
  265.0 0.5 convolution_convert_fusion.1
  265.5 0.3 copy.24
  265.8 59.0 %all_to_all.46 = bf16[16,256,128]{2,1,0:T(8,128)(2,1)S(1)} all-to-all(bf16[16,256,128]{2,1,0:T(8,128)(2,1)S(1)} %copy.24), channel_id=1, replica_groups=mesh['tm'=8,'row'=16,'col'=4] {'tm'}, dimensions={0} | all-to-all | bytes 2097152 | tf_op jit(solution)/shard_map/all_to_all | solution.py:83
  324.8 0.7 copy.34
  325.5 0.5 all_to_all.39
  326.0 1.5 convolution_convert_fusion.2
  327.4 1.0 broadcast_in_dim.2
  328.5 4.8 %all-to-all-start.2 = ((bf16[4,2,256,256]{3,2,1,0:T(8,128)(2,1)}), bf16[4,2,256,256]{3,2,1,0:T(8,128)(2,1)S(1)}, u32[]{:S(2)}, u32[]{:S(2)}) async-start(bf16[4,2,256,256]{3,2,1,0:T(8,128)(2,1)} %broadcast_in_dim.2), calls=%async_computation.2 | async-start | bytes 2097152 | tf_op jit(solution)/shard_map/all_to_all | solution.py:24
  333.3 0.9 slice_convert_fusion
  334.2 10.3 %all-to-all-done.2 = bf16[4,2,256,256]{3,2,1,0:T(8,128)(2,1)S(1)} async-done(((bf16[4,2,256,256]{3,2,1,0:T(8,128)(2,1)}), bf16[4,2,256,256]{3,2,1,0:T(8,128)(2,1)S(1)}, u32[]{:S(2)}, u32[]{:S(2)}) %all-to-all-start.2) | async-done | bytes 1048608 | tf_op jit(solution)/shard_map/all_to_all | solution.py:24
  344.6 0.1 convert_reduce_fusion.1
  344.7 0.5 fusion.4
  345.2 0.5 copy.27
  345.8 1.0 copy.28
  346.8 7.7 %all-to-all-start.3 = ((bf16[16,64,2,256]{3,1,2,0:T(8,128)(2,1)}), bf16[16,64,2,256]{3,1,2,0:T(8,128)(2,1)S(1)}, u32[]{:S(2)}, u32[]{:S(2)}) async-start(bf16[16,64,2,256]{3,1,2,0:T(8,128)(2,1)} %copy.28), calls=%async_computation.3 | async-start | bytes 2097152 | tf_op jit(solution)/shard_map/all_to_all | solution.py:38
  354.5 22.0 %all-to-all-done.3 = bf16[16,64,2,256]{3,1,2,0:T(8,128)(2,1)S(1)} async-done(((bf16[16,64,2,256]{3,1,2,0:T(8,128)(2,1)}), bf16[16,64,2,256]{3,1,2,0:T(8,128)(2,1)S(1)}, u32[]{:S(2)}, u32[]{:S(2)}) %all-to-all-start.3) | async-done | bytes 1048608 | tf_op jit(solution)/shard_map/all_to_all | solution.py:38
  376.5 0.1 convert_reduce_fusion
  376.6 0.8 copy.30
  (6 shorter events, 0.1 us)
Async XLA Ops:
  6.5 139.9 %all-gather.3.cloned.1.call-start = ((), (), s32[]{:S(2)}) async-start(), calls=%async_computation.4 | async-start | bytes 9469952 | tf_op jit(solution)/shard_map/all_gather | solution.py:15
  38.1 149.8 %all-gather.5.cloned.1.call-start = ((), (), s32[]{:S(2)}) async-start(), calls=%async_computation.5 | async-start | bytes 2785280 | tf_op jit(solution)/shard_map/all_gather | solution.py:15
  38.2 112.3 %copy-start.1 = (bf16[64,256]{1,0:T(8,128)(2,1)S(1)}, bf16[64,256]{1,0:T(8,128)(2,1)}, u32[]{:S(2)}) copy-start(bf16[64,256]{1,0:T(8,128)(2,1)} %param.9) | copy-start | bytes 98308
  150.4 1.6 copy-start.2
  150.4 1.6 copy-start.3
  187.9 5.1 %copy-start = (bf16[1024,4352]{1,0:T(8,128)(2,1)S(1)}, bf16[1024,4352]{1,0:T(8,128)(2,1)}, u32[]{:S(2)}) copy-start(bf16[1024,4352]{1,0:T(8,128)(2,1)} %all-gather.3.cloned.1.call-done) | copy-start | bytes 26738692
  193.0 2.7 copy-start.4
  200.4 62.0 %all-to-all-start = ((bf16[2,256,1024]{1,0,2:T(2,128)(2,1)}), bf16[2,256,1024]{1,0,2:T(2,128)(2,1)S(1)}, u32[]{:S(2)}, u32[]{:S(2)}) async-start(bf16[2,256,1024]{1,0,2:T(2,128)(2,1)} %copy.22), calls=%async_computation | async-start | bytes 2097152 | tf_op jit(solution)/shard_map/all_to_all | solution.py:80
  328.5 16.1 %all-to-all-start.2 = ((bf16[4,2,256,256]{3,2,1,0:T(8,128)(2,1)}), bf16[4,2,256,256]{3,2,1,0:T(8,128)(2,1)S(1)}, u32[]{:S(2)}, u32[]{:S(2)}) async-start(bf16[4,2,256,256]{3,2,1,0:T(8,128)(2,1)} %broadcast_in_dim.2), calls=%async_computation.2 | async-start | bytes 2097152 | tf_op jit(solution)/shard_map/all_to_all | solution.py:24
  346.8 29.7 %all-to-all-start.3 = ((bf16[16,64,2,256]{3,1,2,0:T(8,128)(2,1)}), bf16[16,64,2,256]{3,1,2,0:T(8,128)(2,1)S(1)}, u32[]{:S(2)}, u32[]{:S(2)}) async-start(bf16[16,64,2,256]{3,1,2,0:T(8,128)(2,1)} %copy.28), calls=%async_computation.3 | async-start | bytes 2097152 | tf_op jit(solution)/shard_map/all_to_all | solution.py:38
Sparse Core Ops, SparseCore 0:
  38.3 108.1 all-gather.2
  151.5 36.3 all-gather.4
where the time goes:
time: 388 us; the launch traced here: 384 us
  waiting for transfers between devices  224 us (58%)
  blocking collectives  88.2 us (23%)
  starting transfers between devices  25.6 us (7%)
  local copies, waits for them, and re-layouts  15.3 us (4%)
  between operations  13.6 us (4%)
  matrix products  11.7 us (3%)
  other arithmetic  5.93 us (2%)
    all_gather x2, waiting for transfers between devices, sent_together(): lax.all_gather(both, axis, axis=dim, tiled=True)  143 us
    all_to_all x1, blocking collectives, shards(): lax.all_to_all(spectral, 'tm', split_axis=0, concat_axis=2, tiled=True)  59 us
    all_to_all x1, waiting for transfers between devices, shards(): lax.all_to_all(polar, 'tm', split_axis=2, concat_axis=0, tiled=True)  49 us
    all_gather x1, blocking collectives, sent_together(): lax.all_gather(both, axis, axis=dim, tiled=True)  29.1 us
    all_to_all x1, waiting for transfers between devices, sum_at_owner(): lax.all_to_all(parts, axis, split_axis=0, concat_axis=0, tiled=True)  22 us
    all_to_all x1, starting transfers between devices, shards(): lax.all_to_all(polar, 'tm', split_axis=2, concat_axis=0, tiled=True)  13 us
    all_to_all x1, waiting for transfers between devices, sent_to_all(): return lax.all_to_all(copies, axis, split_axis=0, concat_axis=0, tiled=True)  10.3 us
  transfers between devices with their start and end apart: 5, of which 5 were waited for; matrix products, arithmetic and copies ran while one was open for 1% of the time, Pallas kernels for 0%

commit v1 on v0

v1 whole, which is shorter than its diff:
```python
import jax
import jax.numpy as jnp
import numpy as np
from jax import lax
from jax.experimental import pallas as pl
from jax.experimental.pallas import tpu as pltpu
from jax.sharding import PartitionSpec as P

MESH = pl.DeviceIdType.MESH
F32 = jnp.float32
BF16 = jnp.bfloat16
NT = 16
NZ = 16
DAMP = 0.3


def transform_matrix():
    moments = (0.25 * (np.arange(NT) + 0.5)).astype(np.float32)
    omegas = (0.4 * (np.arange(NT) + 0.5)).astype(np.float32)
    cosine = (0.5 * np.cos(omegas[:, None] * moments[None, :])).astype(np.float32)
    order = np.array([2 * tm + e for e in range(2) for tm in range(8)])
    return jnp.asarray(np.kron(cosine[order], np.eye(16)), dtype=BF16)


def kernel(
    occ_ref, emp_ref, x_ref, orate_ref, erate_ref, kron_ref, out_ref,
    colbuf, rowbuf, pk, lhs, acc, pol, spec, xc, fs, f1r, f1s, f2r, mb, yo, ysend, yrecv, zsend, zrecv,
    zag_s, zag_r, zd_s, zd_r, r1_s, r1_r, ag_s, ag_r, rs_s, rs_r, yd_s, yd_r, zr_s, zr_r,
):
    tm, row, y = lax.axis_index("tm"), lax.axis_index("row"), lax.axis_index("col")
    c, zh = tm % 2, tm // 2
    zl, x = row // 4, row % 4
    z = zh * 4 + zl
    u = x * (1 - c) + y * c
    v = y * (1 - c) + x * c

    def at_z(step):
        other = (z + step + NZ) % NZ
        return ((other // 4) * 2 + c, (other % 4) * 4 + x, y)

    def u_peer(d):
        return (tm, zl * 4 + (x + d * (1 - c)) % 4, (y + d * c) % 4)

    def v_peer(d):
        return (tm, zl * 4 + (x + d * c) % 4, (y + d * (1 - c)) % 4)

    partner = (zh * 2 + 1 - c, row, y)

    def remote(src, dst, ss, rs, dev):
        return pltpu.make_async_remote_copy(
            src_ref=src, dst_ref=dst, send_sem=ss, recv_sem=rs, device_id=dev, device_id_type=MESH
        )

    sends = []

    colbuf[c, z, 0:64, :] = occ_ref[...].reshape(64, 256)
    colbuf[c, z, 64:80, :] = x_ref[pl.ds(zh * 2, 2)].reshape(16, 256)
    colbuf[c, z, 80:144, :] = emp_ref[...].reshape(64, 256)
    for t in range(8):
        pk[t, 0] = occ_ref[t]
        pk[t, 1] = emp_ref[t]
    rowbuf[u, v, tm, 0] = occ_ref[tm]
    rowbuf[u, v, tm, 1] = emp_ref[tm]

    barrier = pltpu.get_barrier_semaphore()
    peers = [((tm + d) % 8, row, y) for d in range(1, 8)] + [at_z(1), at_z(-1)]
    peers += [u_peer(d) for d in range(1, 4)] + [v_peer(d) for d in range(1, 4)]
    for peer in peers:
        pl.semaphore_signal(barrier, inc=1, device_id=peer, device_id_type=MESH)
    pl.semaphore_wait(barrier, len(peers))

    halves = (pl.ds(0, 80), pl.ds(80, 64))

    def ring_copy(direction, t, sub):
        owner = (z - t + NZ) % NZ if direction == 0 else (z + t) % NZ
        ref = colbuf.at[c, owner, halves[sub], :]
        return remote(
            ref, ref, zag_s.at[direction, t, sub], zag_r.at[direction, t, sub], at_z(1 if direction == 0 else -1)
        )

    def pass_across(k, owner, sub):
        ref = colbuf.at[c, owner, halves[sub], :]
        copy = remote(ref, ref, zd_s.at[k, sub], zd_r.at[k, sub], partner)
        copy.start()
        sends.append(copy)
        return copy

    steps = (8, 7)
    across = []
    rings = {}
    for sub in range(2):
        for direction in range(2):
            rings[direction, 0, sub] = ring_copy(direction, 0, sub)
            rings[direction, 0, sub].start()
    r1 = []
    for d in range(1, 8):
        to = (tm + d) % 8
        cd = to % 2
        slot = rowbuf.at[x * (1 - cd) + y * cd, y * (1 - cd) + x * cd, tm]
        r1.append(remote(pk.at[to], slot, r1_s.at[d], r1_r.at[d], (to, row, y)))
        r1[-1].start()
    for sub in range(2):
        across.append(pass_across(0, z, sub))

    def ring_step(t):
        for sub in range(2):
            for direction in range(2):
                if t >= steps[direction]:
                    continue
                rings[direction, t, sub].wait_recv()
                if t + 1 < steps[direction]:
                    rings[direction, t + 1, sub] = ring_copy(direction, t + 1, sub)
                    rings[direction, t + 1, sub].start()
                owner = (z - 1 - t + NZ) % NZ if direction == 0 else (z + 1 + t) % NZ
                across.append(pass_across(1 + direction * 8 + t, owner, sub))

    acc[...] = jnp.zeros_like(acc)
    ring_step(0)
    ring_step(1)
    for copy in r1:
        copy.wait_recv()
    own = rowbuf.at[u, v]
    ag1 = [remote(own, own, ag_s.at[0, d], ag_r.at[0, d], v_peer(d)) for d in range(1, 4)]
    for copy in ag1:
        copy.start()
    ring_step(2)
    ring_step(3)
    for copy in ag1:
        copy.wait_recv()
    line = rowbuf.at[u]
    ag2 = [remote(line, line, ag_s.at[1, d], ag_r.at[1, d], u_peer(d)) for d in range(1, 4)]
    for copy in ag2:
        copy.start()
    for t in range(4, 8):
        ring_step(t)
    for copy in ag2:
        copy.wait_recv()
    for copy in across:
        copy.wait_recv()

    moments = 0.25 * (lax.broadcasted_iota(jnp.int32, (NT, 256), 0).astype(F32) + 0.5)

    @pl.loop(0, 8)
    def _(k):
        for s, rate_ref in ((0, orate_ref), (1, erate_ref)):
            weights = jnp.exp(-rate_ref[pl.ds(k, 1), :] * moments)
            rows = rowbuf[:, :, k, s].astype(F32).reshape(128, 256)
            for j in range(NT):
                lhs[s, j * 128 : (j + 1) * 128, :] = (rows * weights[j : j + 1, :]).astype(BF16)
            cols = colbuf[k % 2, pl.ds((k // 2) * 4, 4), s * 80 : s * 80 + 64, :].reshape(256, 256)
            acc[s] += lax.dot_general(
                lhs[s], cols, (((1,), (1,)), ((), ())), preferred_element_type=F32
            )

    for j in range(NT):
        at = pl.ds(j * 128, 128)
        pol[j] = (-2.0 * acc[0, at, :] * acc[1, at, :]).astype(BF16)
    for g in range(8):
        at = slice(g * 16, g * 16 + 16)
        mixed = jnp.dot(kron_ref[...], pol[:, at, :].reshape(256, 256), preferred_element_type=F32)
        spec[:, at, :] = mixed.astype(BF16).reshape(16, 16, 256)

    for h in range(4):
        for l in range(4):
            xc[l * 64 + h * 16 : l * 64 + h * 16 + 16, :] = colbuf[c, h * 4 + l, 64:80, :]

    rs1, rs2, mg1, mg2 = {}, {}, {}, {}
    for e in range(2):
        for k in range(8):
            part = jnp.dot(spec[e * 8 + k], xc[...], preferred_element_type=F32)
            fs[e, :, :, k] = part.reshape(4, 4, 8, 256).astype(BF16)
        rs1[e] = [
            remote(fs.at[e, (u + d) % 4], f1r.at[e, d - 1], rs_s.at[e, 0, d], rs_r.at[e, 0, d], u_peer(d))
            for d in range(1, 4)
        ]
        for copy in rs1[e]:
            copy.start()
    for e in range(2):
        for copy in rs1[e]:
            copy.wait_recv()
        total = fs[e, u].astype(F32)
        for d in range(3):
            total = total + f1r[e, d].astype(F32)
        f1s[e] = total.astype(BF16)
        rs2[e] = [
            remote(f1s.at[e, (v + d) % 4], f2r.at[e, d - 1], rs_s.at[e, 1, d], rs_r.at[e, 1, d], v_peer(d))
            for d in range(1, 4)
        ]
        for copy in rs2[e]:
            copy.start()
    for e in range(2):
        for copy in rs2[e]:
            copy.wait_recv()
        total = f1s[e, v].astype(F32)
        for d in range(3):
            total = total + f2r[e, d].astype(F32)
        mb[e, u, v] = (x_ref[tm].astype(F32)[None] + DAMP * total).astype(BF16)
        ref = mb.at[e, u, v]
        mg1[e] = [remote(ref, ref, rs_s.at[e, 2, d], rs_r.at[e, 2, d], v_peer(d)) for d in range(1, 4)]
        for copy in mg1[e]:
            copy.start()
    for e in range(2):
        for copy in mg1[e]:
            copy.wait_recv()
        ref = mb.at[e, u]
        mg2[e] = [remote(ref, ref, rs_s.at[e, 3, d], rs_r.at[e, 3, d], u_peer(d)) for d in range(1, 4)]
        for copy in mg2[e]:
            copy.start()

    def second(e, k):
        mid = mb[e, :, :, k].astype(F32).reshape(128, 256).astype(BF16)
        return lax.dot_general(
            spec[e * 8 + k], mid, (((0,), (0,)), ((), ())), preferred_element_type=F32
        ).reshape(4, 64, 256)

    def target(direction, t):
        return (z + 8 - t) % NZ if direction == 0 else (z - 7 + t + NZ) % NZ

    zr = {}

    def forward(e, direction, t, value):
        zsend[e, direction, t] = value.astype(BF16)
        zr[e, direction, t] = remote(
            zsend.at[e, direction, t],
            zrecv.at[e, direction, t],
            zr_s.at[e, direction, t],
            zr_r.at[e, direction, t],
            at_z(1 if direction == 0 else -1),
        )
        zr[e, direction, t].start()

    yd = {}
    for e in range(2):
        for copy in mg2[e]:
            copy.wait_recv()
        for h in range(4):
            ysend[e, h * 4 : h * 4 + 4] = second(e, h * 2 + 1 - c).astype(BF16)
        yd[e] = remote(ysend.at[e], yrecv.at[e], yd_s.at[e], yd_r.at[e], partner)
        yd[e].start()
        for h in range(4):
            yo[e, h * 4 : h * 4 + 4] = second(e, h * 2 + c)
        yd[e].wait_recv()
        for direction in range(2):
            d = target(direction, 0)
            forward(e, direction, 0, yo[e, d] + yrecv[e, d].astype(F32))
    for t in range(1, 8):
        for e in range(2):
            for direction in range(2):
                if t >= steps[direction]:
                    continue
                zr[e, direction, t - 1].wait_recv()
                d = target(direction, t)
                forward(
                    e, direction, t,
                    yo[e, d] + yrecv[e, d].astype(F32) + zrecv[e, direction, t - 1].astype(F32),
                )
    for e in range(2):
        zr[e, 0, 7].wait_recv()
        zr[e, 1, 6].wait_recv()
        total = yo[e, z] + yrecv[e, z].astype(F32) + zrecv[e, 0, 7].astype(F32) + zrecv[e, 1, 6].astype(F32)
        out_ref[e] = x_ref[...].reshape(64, 256).astype(F32) + DAMP * total

    for copy in sends:
        copy.wait_send()
    for group in (rings, zr, yd):
        for copy in group.values():
            copy.wait_send()
    for copies in (r1, ag1, ag2, *rs1.values(), *rs2.values(), *mg1.values(), *mg2.values()):
        for copy in copies:
            copy.wait_send()


def shards(occ_orbitals, empty_orbitals, occ_rate, empty_rate, columns):
    vmem = pl.BlockSpec(memory_space=pltpu.VMEM)
    dma = pltpu.SemaphoreType.DMA
    out = pl.pallas_call(
        kernel,
        out_shape=jax.ShapeDtypeStruct((2, 64, 256), F32),
        in_specs=[vmem] * 6,
        out_specs=vmem,
        scratch_shapes=[
            pltpu.VMEM((2, 16, 144, 256), BF16),
            pltpu.VMEM((4, 4, 8, 2, 8, 256), BF16),
            pltpu.VMEM((8, 2, 8, 256), BF16),
            pltpu.VMEM((2, 2048, 256), BF16),
            pltpu.VMEM((2, 2048, 256), F32),
            pltpu.VMEM((16, 128, 256), BF16),
            pltpu.VMEM((16, 128, 256), BF16),
            pltpu.VMEM((256, 256), BF16),
            pltpu.VMEM((2, 4, 4, 8, 8, 256), BF16),
            pltpu.VMEM((2, 3, 4, 8, 8, 256), BF16),
            pltpu.VMEM((2, 4, 8, 8, 256), BF16),
            pltpu.VMEM((2, 3, 8, 8, 256), BF16),
            pltpu.VMEM((2, 4, 4, 8, 8, 256), BF16),
            pltpu.VMEM((2, 16, 64, 256), F32),
            pltpu.VMEM((2, 16, 64, 256), BF16),
            pltpu.VMEM((2, 16, 64, 256), BF16),
            pltpu.VMEM((2, 2, 8, 64, 256), BF16),
            pltpu.VMEM((2, 2, 8, 64, 256), BF16),
            dma((2, 8, 2)), dma((2, 8, 2)),
            dma((16, 2)), dma((16, 2)),
            dma((8,)), dma((8,)),
            dma((2, 4)), dma((2, 4)),
            dma((2, 4, 4)), dma((2, 4, 4)),
            dma((2,)), dma((2,)),
            dma((2, 2, 8)), dma((2, 2, 8)),
        ],
        compiler_params=pltpu.CompilerParams(
            collective_id=0, has_side_effects=True, vmem_limit_bytes=60 * 1024 * 1024
        ),
        name="screen",
    )(
        occ_orbitals.reshape(8, 8, 256),
        empty_orbitals.reshape(8, 8, 256),
        columns.reshape(8, 8, 256),
        occ_rate.reshape(8, 256),
        empty_rate.reshape(8, 256),
        transform_matrix(),
    )
    return jnp.transpose(out, (1, 0, 2))


def solution(mesh):
    placed = (P(("col", "row"), "tm"), P(("col", "row"), "tm"), P(), P(), P(("col", "row"), None))
    return jax.shard_map(
        shards, mesh=mesh, in_specs=placed, out_specs=P(("col", "row"), "tm", None), check_vma=False
    )
```

time: 388 us -> 110 us (0.28)
  the two profiles are of different devices: /device:TPU:1 before, /device:TPU:4 now
where the time goes in v1:
time: 110 us
  Pallas kernels  106 us (96%)
  local copies, waits for them, and re-layouts  3.57 us (3%)
    pallas_call x1, Pallas kernels, shards(): pl.pallas_call(kernel, out_shape=jax.ShapeDtypeStruct((2, 64, 256), F32),...  106 us

profile of v1, /device:TPU:4, one launch (start us, length us, event | category | flops | bytes accessed | tf_op | source)
XLA Modules:
  0.0 110.1 jit_solution(17781988649266655661)
XLA Ops:
  0.0 0.0 copy-start
  0.0 1.3 %reshape.18.orate_ref = f32[8,256]{1,0:T(8,128)} reshape(f32[2048]{0:T(1024)} %param.8) | data formatting | bytes 16384 | tf_op jit(solution)/shard_map/reshape | solution.py:316
  1.3 0.0 copy-done
  1.3 0.6 reshape.19.erate_ref
  1.9 106.5 %screen.1 = f32[2,64,256]{2,1,0:T(8,128)} custom-call(bf16[8,8,256]{2,1,0:T(8,128)(2,1)} %bitcast.5, bf16[8,8,256]{2,1,0:T(8,128)(2,1)} %bitcast.6, bf16[8,8,256]{2,1,0:T(8,128)(2,1)} %bitcast.7, f32[8,256]{1,0:T(8,128)} %reshape.18.orate_ref, f32[8,256]{1,0:T(8,128)} %reshape.19.erate_ref, bf16[256,256]{1,0:T(8,128)(2,1)} %constant.2.clone.kron_ref), custom_call_target="tpu_custom_call" | custom-call | tf_op jit(solution)/shard_map/screen/pallas_call | solution.py:276
  108.4 1.7 %copy.7 = f32[64,2,256]{2,1,0:T(2,128)} copy(f32[64,2,256]{2,0,1:T(8,128)} %bitcast.4) | data formatting | bytes 262144 | tf_op jit(solution)/shard_map/transpose | solution.py:320
Async XLA Ops:
  0.0 1.3 %copy-start = (f32[2048]{0:T(1024)S(1)}, f32[2048]{0:T(1024)}, u32[]{:S(2)}) copy-start(f32[2048]{0:T(1024)} %param.9) | copy-start | bytes 24580

commit v2 on v0

v2 whole, which is shorter than its diff:
```python
import jax
import jax.numpy as jnp
import numpy as np
from jax import lax
from jax.experimental import pallas as pl
from jax.experimental.pallas import tpu as pltpu
from jax.sharding import PartitionSpec as P

MESH = pl.DeviceIdType.MESH
F32 = jnp.float32
BF16 = jnp.bfloat16
NT = 16
NZ = 16
DAMP = 0.3
PIECES = ((0, 80), (80, 64), (144, 64), (208, 64))
OFFSET = ((144, 208), (0, 80))
UP, DOWN = 0, 1


_open = []


def phase(name):
    pass


def transform_matrix():
    moments = (0.25 * (np.arange(NT) + 0.5)).astype(np.float32)
    omegas = (0.4 * (np.arange(NT) + 0.5)).astype(np.float32)
    cosine = (0.5 * np.cos(omegas[:, None] * moments[None, :])).astype(np.float32)
    order = np.array([4 * zh + 2 * c + e for c in range(2) for e in range(2) for zh in range(4)])
    return jnp.asarray(np.kron(cosine[order], np.eye(16)), dtype=BF16)


def kernel(
    occ_ref, emp_ref, x_ref, orate_ref, erate_ref, kron_ref, out_ref,
    colbuf, rowbuf, pk, lhs, acc, pol, spec, xc, fs, f1r, f1s, f2r, mb, yo, ysend, yrecv, yloc, zsend, zrecv,
    zag_s, zag_r, zd_s, zd_r, zo_s, zo_r, r1_s, r1_r, ag1_s, ag1_r, ag2_s, ag2_r, rd_s, rd_r,
    rs_s, rs_r, yd_s, yd_r, yl_s, yl_r, zr_s, zr_r,
):
    tm, row, y = lax.axis_index("tm"), lax.axis_index("row"), lax.axis_index("col")
    c, zh = tm % 2, tm // 2
    zl, x = row // 4, row % 4
    z = zh * 4 + zl
    u = x * (1 - c) + y * c
    v = y * (1 - c) + x * c

    def at_z(step, core):
        other = (z + step + NZ) % NZ
        return ((other // 4) * 2 + core, (other % 4) * 4 + x, y)

    def plane(t, dx, dy):
        return (t, zl * 4 + (x + dx) % 4, (y + dy) % 4)

    def u_peer(d):
        return plane(tm, d * (1 - c), d * c)

    def v_peer(d):
        return plane(tm, d * c, d * (1 - c))

    partner = (zh * 2 + 1 - c, row, y)

    def remote(src, dst, ss, rs, dev):
        return pltpu.make_async_remote_copy(
            src_ref=src, dst_ref=dst, send_sem=ss, recv_sem=rs, device_id=dev, device_id_type=MESH
        )

    for t in range(8):
        pk[t, 0] = occ_ref[t]
        pk[t, 1] = emp_ref[t]

    @pl.when(c == 1)
    def _():
        colbuf[z, 0:64, :] = occ_ref[...].reshape(64, 256)
        colbuf[z, 64:80, :] = x_ref[pl.ds(zh * 2, 2)].reshape(16, 256)
        colbuf[z, 80:144, :] = emp_ref[...].reshape(64, 256)

    @pl.when(c == 0)
    def _():
        colbuf[z, 144:208, :] = occ_ref[...].reshape(64, 256)
        colbuf[z, 208:272, :] = emp_ref[...].reshape(64, 256)
        for h in range(2):
            uh, vh = (x, y) if h == 0 else (y, x)
            rowbuf[h, uh, vh, tm, 0] = occ_ref[zh * 2 + h]
            rowbuf[h, uh, vh, tm, 1] = emp_ref[zh * 2 + h]

    phase("bar")
    barrier = pltpu.get_barrier_semaphore()
    peers = [((tm + d) % 8, row, y) for d in range(1, 8)]
    peers += [at_z(step, core) for step in (1, -1) for core in (0, 1)]
    peers += [u_peer(d) for d in range(1, 4)] + [v_peer(d) for d in range(1, 4)]
    for peer in peers:
        pl.semaphore_signal(barrier, inc=1, device_id=peer, device_id_type=MESH)
    pl.semaphore_wait(barrier, len(peers))

    def to_row_gatherer(d, h):
        to = (zh + d) % 4
        uh, vh = (x, y) if h == 0 else (y, x)
        return remote(
            pk.at[to * 2 + h], rowbuf.at[h, uh, vh, tm], r1_s.at[d, h], r1_r.at[d, c, h], (to * 2, row, y)
        )

    def steps(piece, direction):
        return 8 if (piece < 2) == (direction == UP) else 7

    def shard(owner, piece):
        start, size = PIECES[piece]
        return colbuf.at[owner, pl.ds(start, size), :]

    def ring_copy(direction, t, piece):
        ref = shard((z - t + NZ) % NZ if direction == UP else (z + t) % NZ, piece)
        to = at_z(1 if direction == UP else -1, 1)
        return remote(ref, ref, zag_s.at[direction, t, piece], zag_r.at[direction, t, piece], to)

    def hand_over(direction, t, piece):
        ref = shard((z - 1 - t + NZ) % NZ if direction == UP else (z + 1 + t) % NZ, piece)
        return remote(ref, ref, zd_s.at[direction, t, piece], zd_r.at[direction, t, piece], partner)

    def own_over(piece):
        ref = shard(z, piece)
        return remote(ref, ref, zo_s.at[piece], zo_r.at[piece], partner)

    def row_over(uo, vo, i):
        ref = rowbuf.at[1, uo, vo]
        return remote(ref, ref, rd_s.at[i], rd_r.at[i], partner)

    acc[...] = jnp.zeros_like(acc)

    @pl.when(c == 1)
    def _():
        phase("issue")
        r1 = [to_row_gatherer(d, h) for d in range(4) for h in range(2)]
        started = []

        def start(copy):
            copy.start()
            started.append(copy)

        for copy in r1[2:]:
            start(copy)
        for piece in range(2):
            for direction in (UP, DOWN):
                start(ring_copy(direction, 0, piece))
        for copy in r1[:2]:
            start(copy)
        for piece in range(2):
            start(own_over(piece))
        for piece in range(2, 4):
            own_over(piece).wait_recv()
            for direction in (UP, DOWN):
                start(ring_copy(direction, 0, piece))
        for t in range(8):
            phase(f"z{t}")
            for piece in range(4):
                for direction in (UP, DOWN):
                    if t >= steps(piece, direction):
                        continue
                    ring_copy(direction, t, piece).wait_recv()
                    if t + 1 < steps(piece, direction):
                        start(ring_copy(direction, t + 1, piece))
                    start(hand_over(direction, t, piece))
        phase("roww")
        for i in range(16):
            row_over(0, 0, i).wait_recv()
        phase("sendw")
        for copy in started:
            copy.wait_send()

    @pl.when(c == 0)
    def _():
        phase("issue")
        started = []

        def start(copy):
            copy.start()
            started.append(copy)

        for piece in range(2, 4):
            start(own_over(piece))
        for d in range(1, 4):
            for h in range(2):
                start(to_row_gatherer(d, h))

        def first_stage(h, d):
            ref = rowbuf.at[h, x, y] if h == 0 else rowbuf.at[h, y, x]
            return remote(ref, ref, ag1_s.at[h, d], ag1_r.at[h, d], plane(tm, d * h, d * (1 - h)))

        def second_stage(h, d, back):
            uo, vo = (x, (y - back + 4) % 4) if h == 0 else (y, (x - back + 4) % 4)
            ref = rowbuf.at[h, uo, vo]
            return remote(ref, ref, ag2_s.at[h, d, back], ag2_r.at[h, d, back], plane(tm, d * (1 - h), d * h))

        def rows_over(d, back):
            start(row_over((y - d + 4) % 4, (x - back + 4) % 4, d * 4 + back))

        phase("r1w")
        for h in range(2):
            for core in range(2):
                for d in range(4):
                    if d or core:
                        ref = rowbuf.at[h, 0, 0, 0]
                        remote(ref, ref, r1_s.at[d, h], r1_r.at[d, core, h], partner).wait_recv()
        for h in range(2):
            for d in (2, 1, 3):
                start(first_stage(h, d))
            for d in (2, 1, 3):
                start(second_stage(h, d, 0))
        rows_over(0, 0)
        for back in (1, 3, 2):
            for h in range(2):
                phase(f"ag1w{back}{h}")
                first_stage(h, back).wait_recv()
                for d in (2, 1, 3):
                    start(second_stage(h, d, back))
            rows_over(0, back)
        for back in (0, 1, 3, 2):
            for d in (1, 3, 2):
                for h in (1, 0):
                    phase(f"ag2w{back}{d}{h}")
                    second_stage(h, d, back).wait_recv()
                    if h == 1:
                        rows_over(d, back)
        phase("colw")
        for piece in range(2):
            own_over(piece).wait_recv()
        for t in range(8):
            for piece in range(4):
                for direction in (UP, DOWN):
                    if t < steps(piece, direction):
                        hand_over(direction, t, piece).wait_recv()
        phase("sendw")
        for copy in started:
            copy.wait_send()

    phase("green")
    moments = 0.25 * (lax.broadcasted_iota(jnp.int32, (NT, 128), 0).astype(F32) + 0.5)

    @pl.loop(0, 4)
    def _(b):
        for s, rate_ref in ((0, orate_ref), (1, erate_ref)):
            cols = []
            for k in range(2):
                at = (b * 2 + k) * 2
                weights = jnp.concatenate(
                    [jnp.exp(-rate_ref[pl.ds(at + i, 1), :] * moments) for i in range(2)], axis=1
                )
                rows = rowbuf[c, :, :, b * 2 + k, s].astype(F32).reshape(128, 256)
                for j in range(NT):
                    lhs[s, j * 128 : (j + 1) * 128, k * 256 : (k + 1) * 256] = (
                        rows * weights[j : j + 1, :]
                    ).astype(BF16)
                cols.append(colbuf[pl.ds(b * 4, 4), OFFSET[k][s] : OFFSET[k][s] + 64, :].reshape(256, 256))
            acc[s] += lax.dot_general(
                lhs[s], jnp.concatenate(cols, axis=1), (((1,), (1,)), ((), ())), preferred_element_type=F32
            )

    phase("pol")
    for j in range(NT):
        at = pl.ds(j * 128, 128)
        pol[j] = (-2.0 * acc[0, at, :] * acc[1, at, :]).astype(BF16)
    phase("trans")
    for g in range(8):
        at = slice(g * 16, g * 16 + 16)
        mixed = jnp.dot(kron_ref[...], pol[:, at, :].reshape(256, 256), preferred_element_type=F32)
        spec[:, at, :] = mixed.astype(BF16).reshape(16, 16, 256)
    for h in range(4):
        for i in range(4):
            xc[i * 64 + h * 16 : i * 64 + h * 16 + 16, :] = colbuf[h * 4 + i, 64:80, :]

    def to_sum_u(q, d):
        return remote(fs.at[q, (u + d) % 4], f1r.at[q, d - 1], rs_s.at[q, 0, d], rs_r.at[q, 0, d], u_peer(d))

    def to_sum_v(q, d):
        return remote(f1s.at[q, (v + d) % 4], f2r.at[q, d - 1], rs_s.at[q, 1, d], rs_r.at[q, 1, d], v_peer(d))

    def gather_v(q, d):
        ref = mb.at[q, u, v]
        return remote(ref, ref, rs_s.at[q, 2, d], rs_r.at[q, 2, d], v_peer(d))

    def gather_u(q, d):
        ref = mb.at[q, u]
        return remote(ref, ref, rs_s.at[q, 3, d], rs_r.at[q, 3, d], u_peer(d))

    def all_three(make, q, started):
        for d in (2, 1, 3):
            copy = make(q, d)
            copy.start()
            started.append(copy)

    def arrived(make, q):
        for d in (1, 3, 2):
            make(q, d).wait_recv()

    first_sends = []
    for q in range(4):
        phase(f"first{q}")
        for k in range(4):
            part = jnp.dot(spec[q * 4 + k], xc[...], preferred_element_type=F32)
            fs[q, :, :, k] = part.reshape(4, 4, 8, 256).astype(BF16)
        all_three(to_sum_u, q, first_sends)

    def sum_u(q, started):
        phase(f"rs1w{q}")
        arrived(to_sum_u, q)
        phase(f"rs1c{q}")
        total = fs[q, u].astype(F32)
        for d in range(3):
            total = total + f1r[q, d].astype(F32)
        f1s[q] = total.astype(BF16)
        all_three(to_sum_v, q, started)

    def sum_v(q, started):
        phase(f"rs2w{q}")
        arrived(to_sum_v, q)
        phase(f"rs2c{q}")
        total = f1s[q, v].astype(F32)
        for d in range(3):
            total = total + f2r[q, d].astype(F32)
        mb[q, u, v] = (x_ref[tm].astype(F32)[None] + DAMP * total).astype(BF16)
        all_three(gather_v, q, started)

    def spread_u(q, started):
        phase(f"mg1w{q}")
        arrived(gather_v, q)
        all_three(gather_u, q, started)

    def second(q, k):
        mid = mb[q, :, :, k].astype(F32).reshape(128, 256).astype(BF16)
        return lax.dot_general(
            spec[q * 4 + k], mid, (((0,), (0,)), ((), ())), preferred_element_type=F32
        ).reshape(4, 64, 256)

    def pass_partials(q):
        return remote(ysend.at[q], yrecv.at[q], yd_s.at[q], yd_r.at[q], partner)

    def pass_local(q):
        return remote(ysend.at[q, z], yloc.at[q], yl_s.at[q], yl_r.at[q], partner)

    def sum_steps(q, direction):
        return 8 if (q < 2) == (direction == UP) else 7

    def ring_sum(q, direction, t):
        last = t + 1 == sum_steps(q, direction)
        return remote(
            zsend.at[q, direction, t],
            zrecv.at[q, direction, t],
            zr_s.at[q, direction, t],
            zr_r.at[q, direction, t],
            at_z(1 if direction == UP else -1, 0 if last and q < 2 else 1),
        )

    def finish(q, local):
        up, down = sum_steps(q, UP) - 1, sum_steps(q, DOWN) - 1
        ring_sum(q, UP, up).wait_recv()
        ring_sum(q, DOWN, down).wait_recv()
        total = local + zrecv[q, UP, up].astype(F32) + zrecv[q, DOWN, down].astype(F32)
        out_ref[q % 2] = x_ref[...].reshape(64, 256).astype(F32) + DAMP * total

    def events():
        listed = []
        for q in range(4):
            late = 1.4 * q
            listed += [(4.0 + late, sum_u, q), (6.9 + late, sum_v, q), (9.8 + late, spread_u, q)]
        return listed

    @pl.when(c == 1)
    def _():
        started = []

        def multiply(q, started):
            phase(f"mg2w{q}")
            arrived(gather_u, q)
            phase(f"mg2c{q}")
            for k in range(4):
                part = second(q, k)
                yo[q, k * 4 : k * 4 + 4] = part
            if q < 2:
                ysend[q, z] = yo[q, z].astype(BF16)
                copy = pass_local(q)
                copy.start()
                started.append(copy)

        def ring_step(q, started, t):
            phase(f"zr{t}{q}")
            if t == 0:
                pass_partials(q).wait_recv()
            for direction in (UP, DOWN):
                if t >= sum_steps(q, direction):
                    continue
                d = (
                    (z + sum_steps(q, UP) - t) % NZ
                    if direction == UP
                    else (z - sum_steps(q, DOWN) + t + NZ) % NZ
                )
                value = yo[q, d] + yrecv[q, d].astype(F32)
                if t:
                    ring_sum(q, direction, t - 1).wait_recv()
                    value = value + zrecv[q, direction, t - 1].astype(F32)
                zsend[q, direction, t] = value.astype(BF16)
                copy = ring_sum(q, direction, t)
                copy.start()
                started.append(copy)

        listed = [(at, act, q, ()) for at, act, q in events()]
        for q in range(4):
            late = 1.4 * q
            listed.append((13.8 + late, multiply, q, ()))
            for t in range(8):
                listed.append((15.8 + late + 2.1 * t, ring_step, q, (t,)))
        for _, act, q, more in sorted(listed, key=lambda item: item[0]):
            act(q, started, *more)
        for q in (2, 3):
            phase(f"fin{q}")
            finish(q, yo[q, z] + yrecv[q, z].astype(F32))
        phase("sendw2")
        for copy in started + first_sends:
            copy.wait_send()

    @pl.when(c == 0)
    def _():
        started = []

        def multiply(q, started):
            phase(f"mg2w{q}")
            arrived(gather_u, q)
            phase(f"mg2c{q}")
            for k in range(4):
                ysend[q, k * 4 : k * 4 + 4] = second(q, k).astype(BF16)
            copy = pass_partials(q)
            copy.start()
            started.append(copy)

        listed = events() + [(13.8 + 1.4 * q, multiply, q) for q in range(4)]
        for _, act, q in sorted(listed, key=lambda item: item[0]):
            act(q, started)
        for q in (0, 1):
            phase(f"fin{q}")
            pass_local(q).wait_recv()
            finish(q, ysend[q, z].astype(F32) + yloc[q].astype(F32))
        phase("sendw2")
        for copy in started + first_sends:
            copy.wait_send()

    phase(None)


def shards(occ_orbitals, empty_orbitals, occ_rate, empty_rate, columns):
    vmem = pl.BlockSpec(memory_space=pltpu.VMEM)
    dma = pltpu.SemaphoreType.DMA

    def pair(*shape):
        return [dma(shape), dma(shape)]

    out = pl.pallas_call(
        kernel,
        out_shape=jax.ShapeDtypeStruct((2, 64, 256), F32),
        in_specs=[vmem] * 6,
        out_specs=vmem,
        scratch_shapes=[
            pltpu.VMEM((16, 272, 256), BF16),
            pltpu.VMEM((2, 4, 4, 8, 2, 8, 256), BF16),
            pltpu.VMEM((8, 2, 8, 256), BF16),
            pltpu.VMEM((2, 2048, 512), BF16),
            pltpu.VMEM((2, 2048, 256), F32),
            pltpu.VMEM((16, 128, 256), BF16),
            pltpu.VMEM((16, 128, 256), BF16),
            pltpu.VMEM((256, 256), BF16),
            pltpu.VMEM((4, 4, 4, 4, 8, 256), BF16),
            pltpu.VMEM((4, 3, 4, 4, 8, 256), BF16),
            pltpu.VMEM((4, 4, 4, 8, 256), BF16),
            pltpu.VMEM((4, 3, 4, 8, 256), BF16),
            pltpu.VMEM((4, 4, 4, 4, 8, 256), BF16),
            pltpu.VMEM((4, 16, 64, 256), F32),
            pltpu.VMEM((4, 16, 64, 256), BF16),
            pltpu.VMEM((4, 16, 64, 256), BF16),
            pltpu.VMEM((2, 64, 256), BF16),
            pltpu.VMEM((4, 2, 8, 64, 256), BF16),
            pltpu.VMEM((4, 2, 8, 64, 256), BF16),
            *pair(2, 8, 4),
            *pair(2, 8, 4),
            *pair(4),
            dma((4, 2)), dma((4, 2, 2)),
            *pair(2, 4),
            *pair(2, 4, 4),
            *pair(16),
            *pair(4, 4, 4),
            *pair(4),
            *pair(2),
            *pair(4, 2, 8),
        ],
        compiler_params=pltpu.CompilerParams(
            collective_id=0, has_side_effects=True, vmem_limit_bytes=60 * 1024 * 1024
        ),
        name="screen",
    )(
        occ_orbitals.reshape(8, 8, 256),
        empty_orbitals.reshape(8, 8, 256),
        columns.reshape(8, 8, 256),
        occ_rate.reshape(16, 128),
        empty_rate.reshape(16, 128),
        transform_matrix(),
    )
    return jnp.transpose(out, (1, 0, 2))


def solution(mesh):
    placed = (P(("col", "row"), "tm"), P(("col", "row"), "tm"), P(), P(), P(("col", "row"), None))
    return jax.shard_map(
        shards, mesh=mesh, in_specs=placed, out_specs=P(("col", "row"), "tm", None), check_vma=False
    )
```

time: 388 us -> 103 us (0.27)
  waiting for transfers between devices: 224 us -> 0 us
  Pallas kernels: 0 us -> 101 us
  blocking collectives: 88.2 us -> 0 us
  starting transfers between devices: 25.6 us -> 0 us
  local copies, waits for them, and re-layouts: 15.3 us -> 1.66 us
  between operations: 13.6 us -> 0.01 us
  matrix products: 11.7 us -> 0 us
  other arithmetic: 5.93 us -> 0 us
    all_gather x2 -> x0, waiting for transfers between devices: 143 us -> none  [sent_together(): lax.all_gather(both, axis, axis=dim, tiled=True)]
    pallas_call x0 -> x1, Pallas kernels: none -> 101 us  [shards(): pl.pallas_call(kernel, out_shape=jax.ShapeDtypeStruct((2, 64, 256), F32),...]
    all_to_all x3 -> x0, waiting for transfers between devices: 81.3 us -> none  [the longest x1 49 us: shards(): lax.all_to_all(polar, 'tm', split_axis=2, concat_axis=0, tiled=True)]
    all_to_all x1 -> x0, blocking collectives: 59 us -> none  [shards(): lax.all_to_all(spectral, 'tm', split_axis=0, concat_axis=2, tiled=True)]
    all_gather x1 -> x0, blocking collectives: 29.1 us -> none  [sent_together(): lax.all_gather(both, axis, axis=dim, tiled=True)]
    all_to_all x3 -> x0, starting transfers between devices: 25.5 us -> none  [the longest x1 13 us: shards(): lax.all_to_all(polar, 'tm', split_axis=2, concat_axis=0, tiled=True)]
    dot_general x7 -> x0, matrix products: 11.7 us -> none  [the longest x2 6.59 us: shards(): jnp.einsum('ro,co->rc', scaled_occ, occ_block, preferred_element_type=jnp...]
    slice x2 -> x0, local copies, waits for them, and re-layouts: 4.04 us -> none  [sent_together(): lax.slice_in_dim(result, at, at + a.shape[along], axis=along)]
  transfers between devices with their start and end apart: 5 -> 0, of which waited for: 5 -> 0; matrix products, arithmetic and copies ran while one was open for 1% -> 0% of each run, Pallas kernels for 0% -> 0%
where the time goes in v2:
time: 103 us
  Pallas kernels  101 us (98%)
  local copies, waits for them, and re-layouts  1.66 us (2%)
    pallas_call x1, Pallas kernels, shards(): pl.pallas_call(kernel, out_shape=jax.ShapeDtypeStruct((2, 64, 256), F32),...  101 us

profile of v2, /device:TPU:1, one launch (start us, length us, event | category | flops | bytes accessed | tf_op | source)
XLA Modules:
  0.0 103.0 jit_solution(13068052426100583036)
XLA Ops:
  0.0 101.3 %screen.1 = f32[2,64,256]{2,1,0:T(8,128)} custom-call(bf16[8,8,256]{2,1,0:T(8,128)(2,1)} %bitcast.7, bf16[8,8,256]{2,1,0:T(8,128)(2,1)} %bitcast.8, bf16[8,8,256]{2,1,0:T(8,128)(2,1)} %bitcast.9, f32[16,128]{1,0:T(8,128)} %bitcast.10, f32[16,128]{1,0:T(8,128)} %bitcast.11, bf16[256,256]{1,0:T(8,128)(2,1)} %constant.2.clone.kron_ref), custom_call_target="tpu_custom_call" | custom-call | tf_op jit(solution)/shard_map/screen/pallas_call | solution.py:454
  101.3 1.7 %copy.7 = f32[64,2,256]{2,1,0:T(2,128)} copy(f32[64,2,256]{2,0,1:T(8,128)} %bitcast.6) | data formatting | bytes 262144 | tf_op jit(solution)/shard_map/transpose | solution.py:503

commit v3 on v2

v3 whole, which is shorter than its diff:
```python
import jax
import jax.numpy as jnp
import numpy as np
from jax import lax
from jax.experimental import pallas as pl
from jax.experimental.pallas import tpu as pltpu
from jax.sharding import PartitionSpec as P

MESH = pl.DeviceIdType.MESH
F32 = jnp.float32
BF16 = jnp.bfloat16
NT = 16
NZ = 16
DAMP = 0.3
PIECES = ((0, 10), (10, 8), (18, 8), (26, 8))
OFFSET = ((18, 26), (0, 10))
UP, DOWN = 0, 1


_open = []


def phase(name):
    pass


def transform_matrix():
    moments = (0.25 * (np.arange(NT) + 0.5)).astype(np.float32)
    omegas = (0.4 * (np.arange(NT) + 0.5)).astype(np.float32)
    cosine = (0.5 * np.cos(omegas[:, None] * moments[None, :])).astype(np.float32)
    order = np.array([4 * zh + 2 * c + e for c in range(2) for e in range(2) for zh in range(4)])
    return jnp.asarray(np.kron(cosine[order], np.eye(16)), dtype=BF16)


def kernel(
    occ_in, emp_in, x_in, orate_in, erate_in, kron_in, out_ref,
    x_ref, orate_ref, erate_ref, kron_ref,
    colbuf, rowbuf, pk, lhs, acc, pol, spec, xc, fs, f1r, f1s, f2r, mb, yo, ysend, yrecv, yloc, zsend, zrecv,
    in_s, zag_r, zd_r, zo_r, r1_r, ag1_r, ag2_r, rd_r, gs, rs_r, rs_s, yd_r, yl_r, ys, zr_r, zr_s,
):
    tm, row, y = lax.axis_index("tm"), lax.axis_index("row"), lax.axis_index("col")
    c, zh = tm % 2, tm // 2
    zl, x = row // 4, row % 4
    z = zh * 4 + zl
    u = x * (1 - c) + y * c
    v = y * (1 - c) + x * c

    def at_z(step, core):
        other = (z + step + NZ) % NZ
        return ((other // 4) * 2 + core, (other % 4) * 4 + x, y)

    def plane(t, dx, dy):
        return (t, zl * 4 + (x + dx) % 4, (y + dy) % 4)

    def u_peer(d):
        return plane(tm, d * (1 - c), d * c)

    def v_peer(d):
        return plane(tm, d * c, d * (1 - c))

    partner = (zh * 2 + 1 - c, row, y)

    def remote(src, dst, ss, rs, dev):
        return pltpu.make_async_remote_copy(
            src_ref=src, dst_ref=dst, send_sem=ss, recv_sem=rs, device_id=dev, device_id_type=MESH
        )

    rows_of = [(x, y), (y, x)]
    far = (zh + 2) % 4
    late = [
        pltpu.make_async_copy(src, dst, in_s.at[i])
        for i, (src, dst) in enumerate(
            ((x_in, x_ref), (orate_in, orate_ref), (erate_in, erate_ref), (kron_in, kron_ref))
        )
    ]
    early = []
    for s, src in enumerate((occ_in, emp_in)):
        early.append((src, colbuf.at[z, pl.ds(OFFSET[0][s] * (1 - c) + OFFSET[1][s] * c, 8)]))
        for h in range(2):
            early.append((src.at[far * 2 + h], pk.at[h, s]))
            early.append((src.at[zh * 2 + h], rowbuf.at[h, rows_of[h][0], rows_of[h][1], tm, s]))
    early = [pltpu.make_async_copy(src, dst, in_s.at[4]) for src, dst in early]
    own_x = pltpu.make_async_copy(x_in.at[pl.ds(zh * 2, 2)], colbuf.at[z, pl.ds(8, 2)], in_s.at[5])
    for copy in early:
        copy.start()

    @pl.when(c == 1)
    def _():
        own_x.start()

    for copy in late:
        copy.start()

    phase("bar")
    barrier = pltpu.get_barrier_semaphore()
    peers = [((tm + d) % 8, row, y) for d in range(1, 8)]
    peers += [at_z(step, core) for step in (1, -1) for core in (0, 1)]
    peers += [u_peer(d) for d in range(1, 4)] + [v_peer(d) for d in range(1, 4)]
    for peer in peers:
        pl.semaphore_signal(barrier, inc=1, device_id=peer, device_id_type=MESH)
    everything = ysend.at[0, pl.ds(0, 3)]
    pltpu.make_async_copy(everything, everything, in_s.at[4]).wait()

    @pl.when(c == 1)
    def _():
        own_x.wait()

    pl.semaphore_wait(barrier, len(peers))

    def received(ref, sem):
        remote(ref, ref, gs.at[0], sem, partner).wait_recv()

    def sent(ref, sem):
        remote(ref, ref, sem, zo_r.at[0], partner).wait_send()

    def to_row_gatherer(h):
        slot = rowbuf.at[h, rows_of[h][0], rows_of[h][1], tm]
        return remote(pk.at[h], slot, gs.at[0], r1_r, (far * 2, row, y))

    def steps(piece, direction):
        return 8 if (piece < 2) == (direction == UP) else 7

    def shard(owner, start, size):
        return colbuf.at[owner, pl.ds(start, size)]

    def ring_copy(direction, t, piece):
        ref = shard((z - t + NZ) % NZ if direction == UP else (z + t) % NZ, *PIECES[piece])
        to = at_z(1 if direction == UP else -1, 1)
        return remote(ref, ref, gs.at[1], zag_r.at[direction, t, piece], to)

    def hand_over(direction, t, piece):
        ref = shard((z - 1 - t + NZ) % NZ if direction == UP else (z + 1 + t) % NZ, *PIECES[piece])
        return remote(ref, ref, gs.at[2], zd_r.at[t // 4], partner)

    def own_over(start, size, i):
        ref = shard(z, start, size)
        return remote(ref, ref, gs.at[3], zo_r.at[i], partner)

    def rows_over(block):
        ref = rowbuf.at[1, :, :, pl.ds(block * 2, 2)]
        return remote(ref, ref, gs.at[4], rd_r, partner)

    acc[...] = jnp.zeros_like(acc)

    @pl.when(c == 1)
    def _():
        phase("issue")
        for h in range(2):
            to_row_gatherer(h).start()
        for piece in range(2):
            for direction in (UP, DOWN):
                ring_copy(direction, 0, piece).start()
        own_over(0, 18, 0).start()
        for piece in range(2, 4):
            own_over(*PIECES[piece], piece - 1).wait_recv()
            for direction in (UP, DOWN):
                ring_copy(direction, 0, piece).start()
        for t in range(8):
            phase(f"z{t}")
            for piece in range(4):
                for direction in (UP, DOWN):
                    if t >= steps(piece, direction):
                        continue
                    ring_copy(direction, t, piece).wait_recv()
                    if t + 1 < steps(piece, direction):
                        ring_copy(direction, t + 1, piece).start()
                    hand_over(direction, t, piece).start()
        phase("roww")
        received(rowbuf.at[1], rd_r)
        phase("sendw")
        sent(pk, gs.at[0])
        sent(colbuf.at[pl.ds(0, 15)], gs.at[1])
        sent(colbuf.at[pl.ds(0, 15)], gs.at[2])
        sent(colbuf.at[0, pl.ds(0, 18)], gs.at[3])

    @pl.when(c == 0)
    def _():
        phase("issue")
        for piece in range(2, 4):
            own_over(*PIECES[piece], piece - 1).start()
        for h in range(2):
            to_row_gatherer(h).start()

        def take_rows(owner, source):
            for s in range(2):
                for h in range(2):
                    slot = (h, rows_of[h][0], rows_of[h][1], (owner // 4) * 2 + source, s)
                    rowbuf[slot] = colbuf[owner, OFFSET[source][s] + zh * 2 + h]

        def first_stage(k):
            for d in (2, 1, 3):
                for h in range(2):
                    ref = rowbuf.at[h, rows_of[h][0], rows_of[h][1], pl.ds(((zh + k) % 4) * 2, 2)]
                    remote(ref, ref, gs.at[5], ag1_r.at[k], plane(tm, d * h, d * (1 - h))).start()

        def second_stage(k):
            phase(f"ag1w{k}")
            received(ysend.at[0, pl.ds(0, 3)], ag1_r.at[k])
            for back in range(4):
                for d in (2, 1, 3):
                    for h in range(2):
                        uo, vo = (x, (y - back + 4) % 4) if h == 0 else (y, (x - back + 4) % 4)
                        ref = rowbuf.at[h, uo, vo, pl.ds(((zh + k) % 4) * 2, 2)]
                        remote(ref, ref, gs.at[6], ag2_r.at[k], plane(tm, d * (1 - h), d * h)).start()

        def third_stage(k):
            phase(f"ag2w{k}")
            received(ysend.at[0, pl.ds(0, 12)], ag2_r.at[k])
            rows_over((zh + k) % 4).start()

        own_over(0, 18, 0).wait_recv()
        take_rows(z, 1)
        first_stage(0)
        second_stage(0)
        phase("r1w")
        received(ysend.at[0, 0], r1_r)
        first_stage(2)
        third_stage(0)
        second_stage(2)
        phase("z3w")
        received(colbuf.at[pl.ds(0, 8)], zd_r.at[0])
        for k in (1, 3):
            for source in range(2):
                take_rows((z + 4 * k) % NZ, source)
            first_stage(k)
        third_stage(2)
        for k in (1, 3):
            second_stage(k)
        for k in (1, 3):
            third_stage(k)
        phase("colw")
        received(colbuf.at[pl.ds(0, 7)], zd_r.at[1])
        phase("sendw")
        sent(pk, gs.at[0])
        sent(colbuf.at[0, pl.ds(0, 16)], gs.at[3])
        sent(rowbuf.at[1], gs.at[4])
        sent(ysend.at[0, pl.ds(0, 12)], gs.at[5])
        sent(ysend.at[pl.ds(0, 3)], gs.at[6])

    phase("green")
    for copy in late:
        copy.wait()
    moments = 0.25 * (lax.broadcasted_iota(jnp.int32, (NT, 128), 0).astype(F32) + 0.5)

    @pl.loop(0, 4)
    def _(b):
        for s, rate_ref in ((0, orate_ref), (1, erate_ref)):
            cols = []
            for k in range(2):
                at = (b * 2 + k) * 2
                weights = jnp.concatenate(
                    [jnp.exp(-rate_ref[pl.ds(at + i, 1), :] * moments) for i in range(2)], axis=1
                )
                rows = rowbuf[c, :, :, b * 2 + k, s].astype(F32).reshape(128, 256)
                for j in range(NT):
                    lhs[s, j * 128 : (j + 1) * 128, k * 256 : (k + 1) * 256] = (
                        rows * weights[j : j + 1, :]
                    ).astype(BF16)
                cols.append(colbuf[pl.ds(b * 4, 4), OFFSET[k][s] : OFFSET[k][s] + 8].reshape(256, 256))
            acc[s] += lax.dot_general(
                lhs[s], jnp.concatenate(cols, axis=1), (((1,), (1,)), ((), ())), preferred_element_type=F32
            )

    phase("pol")
    for j in range(NT):
        at = pl.ds(j * 128, 128)
        pol[j] = (-2.0 * acc[0, at, :] * acc[1, at, :]).astype(BF16)
    phase("trans")
    for g in range(8):
        at = slice(g * 16, g * 16 + 16)
        mixed = jnp.dot(kron_ref[...], pol[:, at, :].reshape(256, 256), preferred_element_type=F32)
        spec[:, at, :] = mixed.astype(BF16).reshape(16, 16, 256)
    for h in range(4):
        for i in range(4):
            xc[i * 64 + h * 16 : i * 64 + h * 16 + 16, :] = colbuf[h * 4 + i, 8:10].reshape(16, 256)

    def to_sum_u(q, d):
        return remote(fs.at[q, (u + d) % 4], f1r.at[q, d - 1], rs_s.at[0], rs_r.at[q, 0], u_peer(d))

    def to_sum_v(q, d):
        return remote(f1s.at[q, (v + d) % 4], f2r.at[q, d - 1], rs_s.at[1], rs_r.at[q, 1], v_peer(d))

    def gather_v(q, d):
        ref = mb.at[q, u, v]
        return remote(ref, ref, rs_s.at[2], rs_r.at[q, 2], v_peer(d))

    def gather_u(q, d):
        ref = mb.at[q, u]
        return remote(ref, ref, rs_s.at[3], rs_r.at[q, 3], u_peer(d))

    def all_three(make, q):
        for d in (2, 1, 3):
            make(q, d).start()

    for q in range(4):
        phase(f"first{q}")
        for k in range(4):
            part = jnp.dot(spec[q * 4 + k], xc[...], preferred_element_type=F32)
            fs[q, :, :, k] = part.reshape(4, 4, 8, 256).astype(BF16)
        all_three(to_sum_u, q)

    def sum_u(q):
        phase(f"rs1w{q}")
        received(f1r.at[q], rs_r.at[q, 0])
        phase(f"rs1c{q}")
        total = fs[q, u].astype(F32)
        for d in range(3):
            total = total + f1r[q, d].astype(F32)
        f1s[q] = total.astype(BF16)
        all_three(to_sum_v, q)

    def sum_v(q):
        phase(f"rs2w{q}")
        received(f2r.at[q], rs_r.at[q, 1])
        phase(f"rs2c{q}")
        total = f1s[q, v].astype(F32)
        for d in range(3):
            total = total + f2r[q, d].astype(F32)
        mb[q, u, v] = (x_ref[tm].astype(F32)[None] + DAMP * total).astype(BF16)
        all_three(gather_v, q)

    def spread_u(q):
        phase(f"mg1w{q}")
        received(mb.at[q, 0, pl.ds(0, 3)], rs_r.at[q, 2])
        all_three(gather_u, q)

    def second(q, k):
        mid = mb[q, :, :, k].astype(F32).reshape(128, 256).astype(BF16)
        return lax.dot_general(
            spec[q * 4 + k], mid, (((0,), (0,)), ((), ())), preferred_element_type=F32
        ).reshape(4, 64, 256)

    def pass_partials(q, k):
        at = pl.ds(k * 4, 4)
        return remote(ysend.at[q, at], yrecv.at[q, at], ys.at[0], yd_r.at[q], partner)

    def pass_local(q):
        return remote(ysend.at[q, z], yloc.at[q], ys.at[1], yl_r.at[q], partner)

    def sum_steps(q, direction):
        return 8 if (q < 2) == (direction == UP) else 7

    def ring_sum(q, direction, t):
        last = t + 1 == sum_steps(q, direction)
        return remote(
            zsend.at[q, direction, t],
            zrecv.at[q, direction, t],
            zr_s.at[q],
            zr_r.at[q, direction, t],
            at_z(1 if direction == UP else -1, 0 if last and q < 2 else 1),
        )

    def finish(q, local):
        up, down = sum_steps(q, UP) - 1, sum_steps(q, DOWN) - 1
        ring_sum(q, UP, up).wait_recv()
        ring_sum(q, DOWN, down).wait_recv()
        total = local + zrecv[q, UP, up].astype(F32) + zrecv[q, DOWN, down].astype(F32)
        out_ref[:, q % 2, :] = x_ref[...].reshape(64, 256).astype(F32) + DAMP * total

    def events():
        listed = []
        for q in range(4):
            late = 1.4 * q
            listed += [(4.0 + late, sum_u, q), (6.9 + late, sum_v, q), (9.8 + late, spread_u, q)]
        return listed

    @pl.when(c == 1)
    def _():
        def multiply(q):
            phase(f"mg2w{q}")
            received(mb.at[q, pl.ds(0, 3)], rs_r.at[q, 3])
            phase(f"mg2c{q}")
            for k in range(4):
                part = second(q, k)
                yo[q, k * 4 : k * 4 + 4] = part
            if q < 2:
                ysend[q, z] = yo[q, z].astype(BF16)
                pass_local(q).start()

        def ring_step(q, t):
            phase(f"zr{t}{q}")
            if t == 0:
                received(yrecv.at[q], yd_r.at[q])
            for direction in (UP, DOWN):
                if t >= sum_steps(q, direction):
                    continue
                d = (
                    (z + sum_steps(q, UP) - t) % NZ
                    if direction == UP
                    else (z - sum_steps(q, DOWN) + t + NZ) % NZ
                )
                value = yo[q, d] + yrecv[q, d].astype(F32)
                if t:
                    ring_sum(q, direction, t - 1).wait_recv()
                    value = value + zrecv[q, direction, t - 1].astype(F32)
                zsend[q, direction, t] = value.astype(BF16)
                ring_sum(q, direction, t).start()

        listed = [(at, act, q, ()) for at, act, q in events()]
        for q in range(4):
            late = 1.4 * q
            listed.append((13.8 + late, multiply, q, ()))
            for t in range(8):
                listed.append((15.8 + late + 2.4 * t, ring_step, q, (t,)))
        for _, act, q, more in sorted(listed, key=lambda item: item[0]):
            act(q, *more)
        for q in (2, 3):
            phase(f"fin{q}")
            finish(q, yo[q, z] + yrecv[q, z].astype(F32))
        phase("sendw2")
        for q in range(4):
            sent(ysend.at[0, pl.ds(0, 15)], zr_s.at[q])
        sent(yloc, ys.at[1])

    @pl.when(c == 0)
    def _():
        def multiply(q):
            phase(f"mg2w{q}")
            received(mb.at[q, pl.ds(0, 3)], rs_r.at[q, 3])
            phase(f"mg2c{q}")
            for k in range(4):
                ysend[q, k * 4 : k * 4 + 4] = second(q, k).astype(BF16)
                pass_partials(q, k).start()

        listed = events() + [(13.8 + 1.4 * q, multiply, q) for q in range(4)]
        for _, act, q in sorted(listed, key=lambda item: item[0]):
            act(q)
        for q in (0, 1):
            phase(f"fin{q}")
            pass_local(q).wait_recv()
            finish(q, ysend[q, z].astype(F32) + yloc[q].astype(F32))
        phase("sendw2")
        sent(ysend, ys.at[0])

    for i, ref in enumerate((fs.at[pl.ds(0, 3)], f2r, f2r, fs.at[pl.ds(0, 3)])):
        sent(ref, rs_s.at[i])

    phase(None)


def shards(occ_orbitals, empty_orbitals, occ_rate, empty_rate, columns):
    vmem = pl.BlockSpec(memory_space=pltpu.VMEM)
    dma = pltpu.SemaphoreType.DMA

    out = pl.pallas_call(
        kernel,
        out_shape=jax.ShapeDtypeStruct((64, 2, 256), F32),
        in_specs=[pl.BlockSpec(memory_space=pltpu.HBM)] * 6,
        out_specs=vmem,
        scratch_shapes=[
            pltpu.VMEM((8, 8, 256), BF16),
            pltpu.VMEM((16, 128), F32),
            pltpu.VMEM((16, 128), F32),
            pltpu.VMEM((256, 256), BF16),
            pltpu.VMEM((16, 34, 8, 256), BF16),
            pltpu.VMEM((2, 4, 4, 8, 2, 8, 256), BF16),
            pltpu.VMEM((2, 2, 8, 256), BF16),
            pltpu.VMEM((2, 2048, 512), BF16),
            pltpu.VMEM((2, 2048, 256), F32),
            pltpu.VMEM((16, 128, 256), BF16),
            pltpu.VMEM((16, 128, 256), BF16),
            pltpu.VMEM((256, 256), BF16),
            pltpu.VMEM((4, 4, 4, 4, 8, 256), BF16),
            pltpu.VMEM((4, 3, 4, 4, 8, 256), BF16),
            pltpu.VMEM((4, 4, 4, 8, 256), BF16),
            pltpu.VMEM((4, 3, 4, 8, 256), BF16),
            pltpu.VMEM((4, 4, 4, 4, 8, 256), BF16),
            pltpu.VMEM((4, 16, 64, 256), F32),
            pltpu.VMEM((4, 16, 64, 256), BF16),
            pltpu.VMEM((4, 16, 64, 256), BF16),
            pltpu.VMEM((2, 64, 256), BF16),
            pltpu.VMEM((4, 2, 8, 64, 256), BF16),
            pltpu.VMEM((4, 2, 8, 64, 256), BF16),
            dma((6,)),
            dma((2, 8, 4)),
            dma((2,)),
            dma((3,)),
            dma(()),
            dma((4,)),
            dma((4,)),
            dma(()),
            dma((7,)),
            dma((4, 4)), dma((4,)),
            dma((4,)), dma((2,)), dma((2,)),
            dma((4, 2, 8)), dma((4,)),
        ],
        compiler_params=pltpu.CompilerParams(
            collective_id=0, has_side_effects=True, vmem_limit_bytes=60 * 1024 * 1024
        ),
        name="screen",
    )(
        occ_orbitals.reshape(8, 8, 256),
        empty_orbitals.reshape(8, 8, 256),
        columns.reshape(8, 8, 256),
        occ_rate.reshape(16, 128),
        empty_rate.reshape(16, 128),
        transform_matrix(),
    )
    return out


def solution(mesh):
    placed = (P(("col", "row"), "tm"), P(("col", "row"), "tm"), P(), P(), P(("col", "row"), None))
    return jax.shard_map(
        shards, mesh=mesh, in_specs=placed, out_specs=P(("col", "row"), "tm", None), check_vma=False
    )
```

time: 103 us -> 95.3 us (0.925)
  Pallas kernels: 101 us -> 93.6 us
    pallas_call x1, Pallas kernels: 101 us -> 93.6 us  [shards(): pl.pallas_call(kernel, out_shape=jax.ShapeDtypeStruct((64, 2, 256), F32),...]
    transpose x1 -> x0, local copies, waits for them, and re-layouts: 1.66 us -> none  [shards(): return jnp.transpose(out, (1, 0, 2))]
    unnamed x0 -> x1, local copies, waits for them, and re-layouts: none -> 1.57 us
where the time goes in v3:
time: 95.3 us; the launch traced here: 95.1 us
  Pallas kernels  93.6 us (98%)
  local copies, waits for them, and re-layouts  1.57 us (2%)
    pallas_call x1, Pallas kernels, shards(): pl.pallas_call(kernel, out_shape=jax.ShapeDtypeStruct((64, 2, 256), F32),...  93.6 us

profile of v3, /device:TPU:1, one launch (start us, length us, event | category | flops | bytes accessed | tf_op | source)
XLA Modules:
  0.0 95.1 jit_solution(1468555481069081305)
XLA Ops:
  0.0 93.6 %screen.1 = f32[64,2,256]{2,1,0:T(2,128)} custom-call(bf16[8,8,256]{2,1,0:T(8,128)(2,1)} %bitcast.5, bf16[8,8,256]{2,1,0:T(8,128)(2,1)} %bitcast.6, bf16[8,8,256]{2,1,0:T(8,128)(2,1)} %bitcast.7, f32[16,128]{1,0:T(8,128)} %bitcast.8, f32[16,128]{1,0:T(8,128)} %bitcast.9, bf16[256,256]{1,0:T(8,128)(2,1)} %constant.2.clone.kron_in), custom_call_target="tpu_custom_call" | custom-call | tf_op jit(solution)/shard_map/screen/pallas_call | solution.py:445
  93.6 1.6 %copy.8 = f32[64,2,256]{2,1,0:T(2,128)} copy(f32[64,2,256]{2,1,0:T(2,128)} %screen.1) | data formatting | bytes 262144

commit v4 on v3

--- a/solution.py
+++ b/solution.py
@@ -15,6 +15,8 @@
 PIECES = ((0, 10), (10, 8), (18, 8), (26, 8))
 OFFSET = ((18, 26), (0, 10))
 UP, DOWN = 0, 1
+HOPS = (0, 1, 1, 1, 1, 1, 1, 1, 2)
+SUM_HOPS = ((0, 1, 2, 1, 2, 1, 1, 1, 1), (0, 1, 2, 1, 2, 1, 2, 1, 2))
 
 
 _open = []
@@ -94,8 +96,9 @@
     phase("bar")
     barrier = pltpu.get_barrier_semaphore()
     peers = [((tm + d) % 8, row, y) for d in range(1, 8)]
-    peers += [at_z(step, core) for step in (1, -1) for core in (0, 1)]
+    peers += [at_z(step, core) for step in (1, -1, 2, -2) for core in (0, 1)]
     peers += [u_peer(d) for d in range(1, 4)] + [v_peer(d) for d in range(1, 4)]
+    peers += [plane(tm + 1 - 2 * c, 0, d) for d in range(1, 4)]
     for peer in peers:
         pl.semaphore_signal(barrier, inc=1, device_id=peer, device_id_type=MESH)
     everything = ysend.at[0, pl.ds(0, 3)]
@@ -123,10 +126,16 @@
     def shard(owner, start, size):
         return colbuf.at[owner, pl.ds(start, size)]
 
-    def ring_copy(direction, t, piece):
-        ref = shard((z - t + NZ) % NZ if direction == UP else (z + t) % NZ, *PIECES[piece])
-        to = at_z(1 if direction == UP else -1, 1)
-        return remote(ref, ref, gs.at[1], zag_r.at[direction, t, piece], to)
+    def ring_copy(direction, distance, piece):
+        hop = HOPS[distance]
+        sign = 1 if direction == UP else -1
+        ref = shard((z - sign * (distance - hop) + NZ) % NZ, *PIECES[piece])
+        return remote(ref, ref, gs.at[1], zag_r.at[direction, distance - 1, piece], at_z(sign * hop, 1))
+
+    def pass_on(direction, reached, piece):
+        for distance in (reached + 2, reached + 1):
+            if distance <= steps(piece, direction) and HOPS[distance] == distance - reached:
+                ring_copy(direction, distance, piece).start()
 
     def hand_over(direction, t, piece):
         ref = shard((z - 1 - t + NZ) % NZ if direction == UP else (z + 1 + t) % NZ, *PIECES[piece])
@@ -137,7 +146,7 @@
         return remote(ref, ref, gs.at[3], zo_r.at[i], partner)
 
     def rows_over(block):
-        ref = rowbuf.at[1, :, :, pl.ds(block * 2, 2)]
+        ref = rowbuf.at[1, y, :, pl.ds(block * 2, 2)]
         return remote(ref, ref, gs.at[4], rd_r, partner)
 
     acc[...] = jnp.zeros_like(acc)
@@ -149,21 +158,20 @@
             to_row_gatherer(h).start()
         for piece in range(2):
             for direction in (UP, DOWN):
-                ring_copy(direction, 0, piece).start()
+                pass_on(direction, 0, piece)
         own_over(0, 18, 0).start()
         for piece in range(2, 4):
             own_over(*PIECES[piece], piece - 1).wait_recv()
             for direction in (UP, DOWN):
-                ring_copy(direction, 0, piece).start()
+                pass_on(direction, 0, piece)
         for t in range(8):
             phase(f"z{t}")
             for piece in range(4):
                 for direction in (UP, DOWN):
                     if t >= steps(piece, direction):
                         continue
-                    ring_copy(direction, t, piece).wait_recv()
-                    if t + 1 < steps(piece, direction):
-                        ring_copy(direction, t + 1, piece).start()
+                    ring_copy(direction, t + 1, piece).wait_recv()
+                    pass_on(direction, t + 1, piece)
                     hand_over(direction, t, piece).start()
         phase("roww")
         received(rowbuf.at[1], rd_r)
@@ -201,12 +209,13 @@
                     for h in range(2):
                         uo, vo = (x, (y - back + 4) % 4) if h == 0 else (y, (x - back + 4) % 4)
                         ref = rowbuf.at[h, uo, vo, pl.ds(((zh + k) % 4) * 2, 2)]
-                        remote(ref, ref, gs.at[6], ag2_r.at[k], plane(tm, d * (1 - h), d * h)).start()
+                        arrived = rd_r if h else ag2_r.at[k]
+                        remote(ref, ref, gs.at[6], arrived, plane(tm + h, d * (1 - h), d * h)).start()
+            rows_over((zh + k) % 4).start()
 
         def third_stage(k):
             phase(f"ag2w{k}")
-            received(ysend.at[0, pl.ds(0, 12)], ag2_r.at[k])
-            rows_over((zh + k) % 4).start()
+            received(ysend.at[0, pl.ds(0, 6)], ag2_r.at[k])
 
         own_over(0, 18, 0).wait_recv()
         take_rows(z, 1)
@@ -233,7 +242,7 @@
         phase("sendw")
         sent(pk, gs.at[0])
         sent(colbuf.at[0, pl.ds(0, 16)], gs.at[3])
-        sent(rowbuf.at[1], gs.at[4])
+        sent(rowbuf.at[1, 0], gs.at[4])
         sent(ysend.at[0, pl.ds(0, 12)], gs.at[5])
         sent(ysend.at[pl.ds(0, 3)], gs.at[6])
 
@@ -242,21 +251,22 @@
         copy.wait()
     moments = 0.25 * (lax.broadcasted_iota(jnp.int32, (NT, 128), 0).astype(F32) + 0.5)
 
-    @pl.loop(0, 4)
+    @pl.loop(0, 2)
     def _(b):
         for s, rate_ref in ((0, orate_ref), (1, erate_ref)):
             cols = []
-            for k in range(2):
-                at = (b * 2 + k) * 2
+            for k in range(4):
+                at = (b * 4 + k) * 2
                 weights = jnp.concatenate(
                     [jnp.exp(-rate_ref[pl.ds(at + i, 1), :] * moments) for i in range(2)], axis=1
                 )
-                rows = rowbuf[c, :, :, b * 2 + k, s].astype(F32).reshape(128, 256)
+                rows = rowbuf[c, :, :, b * 4 + k, s].astype(F32).reshape(128, 256)
                 for j in range(NT):
                     lhs[s, j * 128 : (j + 1) * 128, k * 256 : (k + 1) * 256] = (
                         rows * weights[j : j + 1, :]
                     ).astype(BF16)
-                cols.append(colbuf[pl.ds(b * 4, 4), OFFSET[k][s] : OFFSET[k][s] + 8].reshape(256, 256))
+                first = OFFSET[k % 2][s]
+                cols.append(colbuf[pl.ds(b * 8 + k // 2 * 4, 4), first : first + 8].reshape(256, 256))
             acc[s] += lax.dot_general(
                 lhs[s], jnp.concatenate(cols, axis=1), (((1,), (1,)), ((), ())), preferred_element_type=F32
             )
@@ -340,21 +350,35 @@
     def sum_steps(q, direction):
         return 8 if (q < 2) == (direction == UP) else 7
 
-    def ring_sum(q, direction, t):
-        last = t + 1 == sum_steps(q, direction)
+    def sum_hop(q, distance):
+        return SUM_HOPS[q // 2][distance]
+
+    def sources(q, direction, left):
+        return [d for d in range(8, 0, -1) if d <= sum_steps(q, direction) and d - sum_hop(q, d) == left]
+
+    def ready(q, direction, left):
+        after = [ready(q, direction, d) + 1.75 + 0.7 * sum_hop(q, d) for d in sources(q, direction, left)]
+        return max(after, default=0.0)
+
+    def ring_sum(q, direction, distance):
+        hop = sum_hop(q, distance)
+        sign = 1 if direction == UP else -1
         return remote(
-            zsend.at[q, direction, t],
-            zrecv.at[q, direction, t],
+            zsend.at[q, direction, distance - 1],
+            zrecv.at[q, direction, distance - 1],
             zr_s.at[q],
-            zr_r.at[q, direction, t],
-            at_z(1 if direction == UP else -1, 0 if last and q < 2 else 1),
+            zr_r.at[q, direction, distance - 1],
+            at_z(sign * hop, 0 if hop == distance and q < 2 else 1),
         )
 
+    def ring_arrived(q, direction, left, value):
+        for d in sources(q, direction, left):
+            ring_sum(q, direction, d).wait_recv()
+            value = value + zrecv[q, direction, d - 1].astype(F32)
+        return value
+
     def finish(q, local):
-        up, down = sum_steps(q, UP) - 1, sum_steps(q, DOWN) - 1
-        ring_sum(q, UP, up).wait_recv()
-        ring_sum(q, DOWN, down).wait_recv()
-        total = local + zrecv[q, UP, up].astype(F32) + zrecv[q, DOWN, down].astype(F32)
+        total = ring_arrived(q, DOWN, 0, ring_arrived(q, UP, 0, local))
         out_ref[:, q % 2, :] = x_ref[...].reshape(64, 256).astype(F32) + DAMP * total
 
     def events():
@@ -377,31 +401,28 @@
                 ysend[q, z] = yo[q, z].astype(BF16)
                 pass_local(q).start()
 
-        def ring_step(q, t):
-            phase(f"zr{t}{q}")
-            if t == 0:
-                received(yrecv.at[q], yd_r.at[q])
-            for direction in (UP, DOWN):
-                if t >= sum_steps(q, direction):
-                    continue
-                d = (
-                    (z + sum_steps(q, UP) - t) % NZ
-                    if direction == UP
-                    else (z - sum_steps(q, DOWN) + t + NZ) % NZ
-                )
-                value = yo[q, d] + yrecv[q, d].astype(F32)
-                if t:
-                    ring_sum(q, direction, t - 1).wait_recv()
-                    value = value + zrecv[q, direction, t - 1].astype(F32)
-                zsend[q, direction, t] = value.astype(BF16)
-                ring_sum(q, direction, t).start()
+        def take_partials(q):
+            phase(f"yw{q}")
+            received(yrecv.at[q], yd_r.at[q])
+
+        def ring_step(q, direction, distance):
+            phase(f"zr{distance}{q}")
+            sign = 1 if direction == UP else -1
+            d = (z + sign * distance + NZ) % NZ
+            value = ring_arrived(q, direction, distance, yo[q, d] + yrecv[q, d].astype(F32))
+            zsend[q, direction, distance - 1] = value.astype(BF16)
+            ring_sum(q, direction, distance).start()
 
         listed = [(at, act, q, ()) for at, act, q in events()]
         for q in range(4):
             late = 1.4 * q
             listed.append((13.8 + late, multiply, q, ()))
-            for t in range(8):
-                listed.append((15.8 + late + 2.4 * t, ring_step, q, (t,)))
+            listed.append((15.8 + late, take_partials, q, ()))
+            for distance in range(8, 0, -1):
+                for direction in (UP, DOWN):
+                    if distance <= sum_steps(q, direction):
+                        at = 15.8 + late + ready(q, direction, distance)
+                        listed.append((at, ring_step, q, (direction, distance)))
         for _, act, q, more in sorted(listed, key=lambda item: item[0]):
             act(q, *more)
         for q in (2, 3):
@@ -455,7 +476,7 @@
             pltpu.VMEM((16, 34, 8, 256), BF16),
             pltpu.VMEM((2, 4, 4, 8, 2, 8, 256), BF16),
             pltpu.VMEM((2, 2, 8, 256), BF16),
-            pltpu.VMEM((2, 2048, 512), BF16),
+            pltpu.VMEM((2, 2048, 1024), BF16),
             pltpu.VMEM((2, 2048, 256), F32),
             pltpu.VMEM((16, 128, 256), BF16),
             pltpu.VMEM((16, 128, 256), BF16),
@@ -485,16 +506,21 @@
             dma((4, 2, 8)), dma((4,)),
         ],
         compiler_params=pltpu.CompilerParams(
-            collective_id=0, has_side_effects=True, vmem_limit_bytes=60 * 1024 * 1024
+            collective_id=0, has_side_effects=True, vmem_limit_bytes=48 * 1024 * 1024
         ),
         name="screen",
     )(
-        occ_orbitals.reshape(8, 8, 256),
-        empty_orbitals.reshape(8, 8, 256),
-        columns.reshape(8, 8, 256),
-        occ_rate.reshape(16, 128),
-        empty_rate.reshape(16, 128),
-        transform_matrix(),
+        *(
+            pltpu.with_memory_space_constraint(a, pltpu.HBM)
+            for a in (
+                occ_orbitals.reshape(8, 8, 256),
+                empty_orbitals.reshape(8, 8, 256),
+                columns.reshape(8, 8, 256),
+                occ_rate.reshape(16, 128),
+                empty_rate.reshape(16, 128),
+                transform_matrix(),
+            )
+        )
     )
     return out
 

time: 95.3 us -> 88.5 us (0.929)
  Pallas kernels: 93.6 us -> 87.7 us
    pallas_call x1, Pallas kernels: 93.6 us -> 87.7 us  [shards(): pl.pallas_call(kernel, out_shape=jax.ShapeDtypeStruct((64, 2, 256), F32),...]
where the time goes in v4:
time: 88.5 us; the launch traced here: 88.4 us
  Pallas kernels  87.7 us (99%)
    pallas_call x1, Pallas kernels, shards(): pl.pallas_call(kernel, out_shape=jax.ShapeDtypeStruct((64, 2, 256), F32),...  87.7 us

profile of v4, /device:TPU:1, one launch (start us, length us, event | category | flops | bytes accessed | tf_op | source)
XLA Modules:
  0.0 88.4 jit_solution(8010851415867088781)
XLA Ops:
  0.0 87.7 %screen.1 = f32[64,2,256]{2,1,0:T(2,128)S(1)} custom-call(bf16[8,8,256]{2,1,0:T(8,128)(2,1)} %bitcast.5, bf16[8,8,256]{2,1,0:T(8,128)(2,1)} %bitcast.6, bf16[8,8,256]{2,1,0:T(8,128)(2,1)} %bitcast.7, f32[16,128]{1,0:T(8,128)} %bitcast.8, f32[16,128]{1,0:T(8,128)} %bitcast.9, bf16[256,256]{1,0:T(8,128)(2,1)} %constant.2.clone.kron_in), custom_call_target="tpu_custom_call" | custom-call | tf_op jit(solution)/shard_map/screen/pallas_call | solution.py:466
  87.7 0.7 copy.8

commit v5 on v4

--- a/solution.py
+++ b/solution.py
@@ -99,6 +99,7 @@
     peers += [at_z(step, core) for step in (1, -1, 2, -2) for core in (0, 1)]
     peers += [u_peer(d) for d in range(1, 4)] + [v_peer(d) for d in range(1, 4)]
     peers += [plane(tm + 1 - 2 * c, 0, d) for d in range(1, 4)]
+    peers += [plane(tm + 1 - 2 * c, d, 0) for d in range(1, 4)]
     for peer in peers:
         pl.semaphore_signal(barrier, inc=1, device_id=peer, device_id_type=MESH)
     everything = ysend.at[0, pl.ds(0, 3)]
@@ -285,57 +286,58 @@
             xc[i * 64 + h * 16 : i * 64 + h * 16 + 16, :] = colbuf[h * 4 + i, 8:10].reshape(16, 256)
 
     def to_sum_u(q, d):
-        return remote(fs.at[q, (u + d) % 4], f1r.at[q, d - 1], rs_s.at[0], rs_r.at[q, 0], u_peer(d))
-
-    def to_sum_v(q, d):
-        return remote(f1s.at[q, (v + d) % 4], f2r.at[q, d - 1], rs_s.at[1], rs_r.at[q, 1], v_peer(d))
-
-    def gather_v(q, d):
-        ref = mb.at[q, u, v]
-        return remote(ref, ref, rs_s.at[2], rs_r.at[q, 2], v_peer(d))
-
-    def gather_u(q, d):
-        ref = mb.at[q, u]
-        return remote(ref, ref, rs_s.at[3], rs_r.at[q, 3], u_peer(d))
-
-    def all_three(make, q):
-        for d in (2, 1, 3):
-            make(q, d).start()
+        to = plane(zh * 2 + 1, d * (1 - c), d * c)
+        return remote(fs.at[q, (u + d) % 4], f1r.at[c, q, d], rs_s.at[0], rs_r.at[c, q, 0], to)
+
+    def along_v(src, dst, stage, h, q, d):
+        plane_v = plane(tm, d * h, d * (1 - h))
+        remote(src, dst, rs_s.at[stage], rs_r.at[h, q, stage], plane_v).start()
 
     for q in range(4):
         phase(f"first{q}")
         for k in range(4):
             part = jnp.dot(spec[q * 4 + k], xc[...], preferred_element_type=F32)
             fs[q, :, :, k] = part.reshape(4, 4, 8, 256).astype(BF16)
-        all_three(to_sum_u, q)
-
-    def sum_u(q):
-        phase(f"rs1w{q}")
-        received(f1r.at[q], rs_r.at[q, 0])
-        phase(f"rs1c{q}")
-        total = fs[q, u].astype(F32)
+        for d in (2, 1, 3):
+            to_sum_u(q, d).start()
+
+        @pl.when(c == 0)
+        def _(q=q):
+            to_sum_u(q, 0).start()
+
+    def sum_u(q, h):
+        phase(f"rs1w{q}{h}")
+        received(f1r.at[1, q, pl.ds(1, 3)] if h else f1r.at[0, q], rs_r.at[h, q, 0])
+        total = (fs[q, u] if h else f1r[0, q, 0]).astype(F32)
+        for d in range(1, 4):
+            total = total + f1r[h, q, d].astype(F32)
+        f1s[h, q] = total.astype(BF16)
+        for d in (2, 1, 3):
+            along_v(f1s.at[h, q, (rows_of[h][1] + d) % 4], f2r.at[h, q, d - 1], 1, h, q, d)
+
+    def sum_v(q, h):
+        phase(f"rs2w{q}{h}")
+        received(f2r.at[h, q], rs_r.at[h, q, 1])
+        total = f1s[h, q, rows_of[h][1]].astype(F32)
         for d in range(3):
-            total = total + f1r[q, d].astype(F32)
-        f1s[q] = total.astype(BF16)
-        all_three(to_sum_v, q)
-
-    def sum_v(q):
-        phase(f"rs2w{q}")
-        received(f2r.at[q], rs_r.at[q, 1])
-        phase(f"rs2c{q}")
-        total = f1s[q, v].astype(F32)
-        for d in range(3):
-            total = total + f2r[q, d].astype(F32)
-        mb[q, u, v] = (x_ref[tm].astype(F32)[None] + DAMP * total).astype(BF16)
-        all_three(gather_v, q)
-
-    def spread_u(q):
-        phase(f"mg1w{q}")
-        received(mb.at[q, 0, pl.ds(0, 3)], rs_r.at[q, 2])
-        all_three(gather_u, q)
+            total = total + f2r[h, q, d].astype(F32)
+        mb[h, q, rows_of[h][0], rows_of[h][1]] = (
+            x_ref[zh * 2 + h].astype(F32)[None] + DAMP * total
+        ).astype(BF16)
+        ref = mb.at[h, q, rows_of[h][0], rows_of[h][1]]
+        for d in (2, 1, 3):
+            along_v(ref, ref, 2, h, q, d)
+
+    def spread_u(q, h):
+        phase(f"mg1w{q}{h}")
+        received(mb.at[0, 0, 0, pl.ds(0, 3)], rs_r.at[h, q, 2])
+        ref = mb.at[h, q, rows_of[h][0]]
+        for d in (2, 1, 3) if h else (2, 1, 3, 0):
+            to = plane(tm, 0, d) if h else plane(tm - 1, d, 0)
+            remote(ref, ref, rs_s.at[3 + (1 - h)], rs_r.at[h, q, 3], to).start()
 
     def second(q, k):
-        mid = mb[q, :, :, k].astype(F32).reshape(128, 256).astype(BF16)
+        mid = mb[c, q, :, :, k].astype(F32).reshape(128, 256).astype(BF16)
         return lax.dot_general(
             spec[q * 4 + k], mid, (((0,), (0,)), ((), ())), preferred_element_type=F32
         ).reshape(4, 64, 256)
@@ -384,15 +386,17 @@
     def events():
         listed = []
         for q in range(4):
-            late = 1.4 * q
-            listed += [(4.0 + late, sum_u, q), (6.9 + late, sum_v, q), (9.8 + late, spread_u, q)]
+            for h in range(2):
+                late = 1.4 * q + 0.2 * (1 - h)
+                for at, act in ((4.0, sum_u), (6.9, sum_v), (9.8, spread_u)):
+                    listed.append((at + late, act, q, (h,)))
         return listed
 
     @pl.when(c == 1)
     def _():
         def multiply(q):
             phase(f"mg2w{q}")
-            received(mb.at[q, pl.ds(0, 3)], rs_r.at[q, 3])
+            received(mb.at[1, q, pl.ds(0, 3)], rs_r.at[1, q, 3])
             phase(f"mg2c{q}")
             for k in range(4):
                 part = second(q, k)
@@ -413,7 +417,7 @@
             zsend[q, direction, distance - 1] = value.astype(BF16)
             ring_sum(q, direction, distance).start()
 
-        listed = [(at, act, q, ()) for at, act, q in events()]
+        listed = events()
         for q in range(4):
             late = 1.4 * q
             listed.append((13.8 + late, multiply, q, ()))
@@ -432,29 +436,28 @@
         for q in range(4):
             sent(ysend.at[0, pl.ds(0, 15)], zr_s.at[q])
         sent(yloc, ys.at[1])
+        for i, ref in enumerate((fs.at[pl.ds(0, 3)], f2r, f2r, fs.at[pl.ds(0, 3)], fs)):
+            sent(ref, rs_s.at[i])
 
     @pl.when(c == 0)
     def _():
         def multiply(q):
             phase(f"mg2w{q}")
-            received(mb.at[q, pl.ds(0, 3)], rs_r.at[q, 3])
+            received(mb.at[0, q], rs_r.at[0, q, 3])
             phase(f"mg2c{q}")
             for k in range(4):
                 ysend[q, k * 4 : k * 4 + 4] = second(q, k).astype(BF16)
                 pass_partials(q, k).start()
 
-        listed = events() + [(13.8 + 1.4 * q, multiply, q) for q in range(4)]
-        for _, act, q in sorted(listed, key=lambda item: item[0]):
-            act(q)
+        for q in range(4):
+            multiply(q)
         for q in (0, 1):
             phase(f"fin{q}")
             pass_local(q).wait_recv()
             finish(q, ysend[q, z].astype(F32) + yloc[q].astype(F32))
         phase("sendw2")
         sent(ysend, ys.at[0])
-
-    for i, ref in enumerate((fs.at[pl.ds(0, 3)], f2r, f2r, fs.at[pl.ds(0, 3)])):
-        sent(ref, rs_s.at[i])
+        sent(fs, rs_s.at[0])
 
     phase(None)
 
@@ -482,10 +485,10 @@
             pltpu.VMEM((16, 128, 256), BF16),
             pltpu.VMEM((256, 256), BF16),
             pltpu.VMEM((4, 4, 4, 4, 8, 256), BF16),
-            pltpu.VMEM((4, 3, 4, 4, 8, 256), BF16),
-            pltpu.VMEM((4, 4, 4, 8, 256), BF16),
-            pltpu.VMEM((4, 3, 4, 8, 256), BF16),
-            pltpu.VMEM((4, 4, 4, 4, 8, 256), BF16),
+            pltpu.VMEM((2, 4, 4, 4, 4, 8, 256), BF16),
+            pltpu.VMEM((2, 4, 4, 4, 8, 256), BF16),
+            pltpu.VMEM((2, 4, 3, 4, 8, 256), BF16),
+            pltpu.VMEM((2, 4, 4, 4, 4, 8, 256), BF16),
             pltpu.VMEM((4, 16, 64, 256), F32),
             pltpu.VMEM((4, 16, 64, 256), BF16),
             pltpu.VMEM((4, 16, 64, 256), BF16),
@@ -501,7 +504,7 @@
             dma((4,)),
             dma(()),
             dma((7,)),
-            dma((4, 4)), dma((4,)),
+            dma((2, 4, 4)), dma((5,)),
             dma((4,)), dma((2,)), dma((2,)),
             dma((4, 2, 8)), dma((4,)),
         ],

time: 88.5 us -> 85.7 us (0.968)
  Pallas kernels: 87.7 us -> 84.9 us
    pallas_call x1, Pallas kernels: 87.7 us -> 84.9 us  [shards(): pl.pallas_call(kernel, out_shape=jax.ShapeDtypeStruct((64, 2, 256), F32),...]
where the time goes in v5:
time: 85.7 us; the launch traced here: 85.5 us
  Pallas kernels  84.9 us (99%)
    pallas_call x1, Pallas kernels, shards(): pl.pallas_call(kernel, out_shape=jax.ShapeDtypeStruct((64, 2, 256), F32),...  84.9 us

profile of v5, /device:TPU:1, one launch (start us, length us, event | category | flops | bytes accessed | tf_op | source)
XLA Modules:
  0.0 85.5 jit_solution(12099118051297273034)
XLA Ops:
  0.0 84.9 %screen.1 = f32[64,2,256]{2,1,0:T(2,128)S(1)} custom-call(bf16[8,8,256]{2,1,0:T(8,128)(2,1)} %bitcast.5, bf16[8,8,256]{2,1,0:T(8,128)(2,1)} %bitcast.6, bf16[8,8,256]{2,1,0:T(8,128)(2,1)} %bitcast.7, f32[16,128]{1,0:T(8,128)} %bitcast.8, f32[16,128]{1,0:T(8,128)} %bitcast.9, bf16[256,256]{1,0:T(8,128)(2,1)} %constant.2.clone.kron_in), custom_call_target="tpu_custom_call" | custom-call | tf_op jit(solution)/shard_map/screen/pallas_call | solution.py:469
  84.9 0.7 copy.8

commit v6 on v5

--- a/solution.py
+++ b/solution.py
@@ -16,7 +16,8 @@
 OFFSET = ((18, 26), (0, 10))
 UP, DOWN = 0, 1
 HOPS = (0, 1, 1, 1, 1, 1, 1, 1, 2)
-SUM_HOPS = ((0, 1, 2, 1, 2, 1, 1, 1, 1), (0, 1, 2, 1, 2, 1, 2, 1, 2))
+EVEN = (0, 1, 2, 1, 2, 1, 2, 1, 2)
+SUM_HOPS = ((0, 1, 2, 1, 2, 1, 1, 1, 1), (0, 1, 2, 1, 2, 1, 1, 1, 2), EVEN, EVEN)
 
 
 _open = []
@@ -95,7 +96,7 @@
 
     phase("bar")
     barrier = pltpu.get_barrier_semaphore()
-    peers = [((tm + d) % 8, row, y) for d in range(1, 8)]
+    peers = [partner, (far * 2, row, y), (far * 2 + 1, row, y)]
     peers += [at_z(step, core) for step in (1, -1, 2, -2) for core in (0, 1)]
     peers += [u_peer(d) for d in range(1, 4)] + [v_peer(d) for d in range(1, 4)]
     peers += [plane(tm + 1 - 2 * c, 0, d) for d in range(1, 4)]
@@ -353,7 +354,7 @@
         return 8 if (q < 2) == (direction == UP) else 7
 
     def sum_hop(q, distance):
-        return SUM_HOPS[q // 2][distance]
+        return SUM_HOPS[q][distance]
 
     def sources(q, direction, left):
         return [d for d in range(8, 0, -1) if d <= sum_steps(q, direction) and d - sum_hop(q, d) == left]

time: 85.7 us -> 86.6 us (1.011)
  Pallas kernels: 84.9 us -> 85.8 us
    pallas_call x1, Pallas kernels: 84.9 us -> 85.8 us  [shards(): pl.pallas_call(kernel, out_shape=jax.ShapeDtypeStruct((64, 2, 256), F32),...]
where the time goes in v6:
time: 86.6 us; the launch traced here: 86.5 us
  Pallas kernels  85.8 us (99%)
    pallas_call x1, Pallas kernels, shards(): pl.pallas_call(kernel, out_shape=jax.ShapeDtypeStruct((64, 2, 256), F32),...  85.8 us

profile of v6, /device:TPU:1, one launch (start us, length us, event | category | flops | bytes accessed | tf_op | source)
XLA Modules:
  0.0 86.5 jit_solution(10191931803593054668)
XLA Ops:
  0.0 85.8 %screen.1 = f32[64,2,256]{2,1,0:T(2,128)S(1)} custom-call(bf16[8,8,256]{2,1,0:T(8,128)(2,1)} %bitcast.5, bf16[8,8,256]{2,1,0:T(8,128)(2,1)} %bitcast.6, bf16[8,8,256]{2,1,0:T(8,128)(2,1)} %bitcast.7, f32[16,128]{1,0:T(8,128)} %bitcast.8, f32[16,128]{1,0:T(8,128)} %bitcast.9, bf16[256,256]{1,0:T(8,128)(2,1)} %constant.2.clone.kron_in), custom_call_target="tpu_custom_call" | custom-call | tf_op jit(solution)/shard_map/screen/pallas_call | solution.py:470
  85.8 0.7 copy.8
